TPU v7x, 8 devices: a whole 2x2x1 slice. The times are simulated.
8 devices in a mesh: dp: 2 (over z, y), ep: 4 (over x, core).
Axes of the slice: x: 2, y: 2, z: 1, core: 2. Of those that a mesh axis runs over, the one named last changes fastest.
Arguments:
- x_tokens: bfloat16 [512, 1024], P(('dp', 'ep')), parts along dimension 0
- dy_tokens: bfloat16 [512, 1024], P(('dp', 'ep')), parts along dimension 0
- expert_ids: int32 [512, 8], P(('dp', 'ep')), parts along dimension 0
- gate_vals: float32 [512, 8], P(('dp', 'ep')), parts along dimension 0
- slot_ids: int32 [512, 8], P(('dp', 'ep')), parts along dimension 0
- w_gate: bfloat16 [32, 1024, 512], P('ep')
- w_down: bfloat16 [32, 512, 1024], P('ep')
- w_up: bfloat16 [32, 1024, 512], P('ep')
Outputs:
- output 1: bfloat16 [512, 1024], P(('dp', 'ep')), parts along dimension 0
- output 2: float32 [64, 1024, 512], P(('dp', 'ep')), parts along dimension 0
- output 3: float32 [64, 512, 1024], P(('dp', 'ep')), parts along dimension 0
- output 4: float32 [64, 1024, 512], P(('dp', 'ep')), parts along dimension 0
There are 2 independent parts. A program takes and returns all parts, laid end to end along the dimension named above; an argument that names none is the same for every part.
All inputs are finite; a program needn't handle non-finite values.
Results may differ from a plain program's by a relative error of at most 0.0103763.
Values are sent between devices in bfloat16 or wider.
A program may use at most 1 GiB of HBM per device.

v0:
```python
import jax
import jax.numpy as jnp
from jax import lax
from jax.sharding import PartitionSpec as P


def slot_capacity(tok_dev, top_k, n_exp):
    return ((3 * tok_dev * top_k) // (2 * n_exp) + 7) // 8 * 8


def source_dispatch(x_src, dy_src, ids_src, gate_src, slot_src, cap_rows, n_exp):
    tok_dev, top_k = ids_src.shape
    n_copy = tok_dev * top_k
    d_model = x_src.shape[1]
    flat_slot = jnp.where(slot_src >= 0, ids_src * cap_rows + slot_src, n_exp * cap_rows)
    slot_copy = jnp.full((n_exp * cap_rows,), n_copy, jnp.int32).at[flat_slot.reshape(n_copy)].set(jnp.arange(n_copy, dtype=jnp.int32), mode='drop')
    slot_tok = slot_copy // top_k
    x_send = jnp.take(x_src, slot_tok, axis=0, mode='fill', fill_value=0)
    dy_send = jnp.take(dy_src, slot_tok, axis=0, mode='fill', fill_value=0)
    gate_slot = jnp.take(gate_src.reshape(n_copy), slot_copy, mode='fill', fill_value=0)
    dz_send = (gate_slot[:, None] * dy_send).astype(jnp.bfloat16)
    return x_send.reshape(n_exp, cap_rows, d_model), dz_send.reshape(n_exp, cap_rows, d_model), flat_slot


def source_combine(dx_send, flat_slot):
    n_exp, cap_rows, d_model = dx_send.shape
    rows = jnp.take(dx_send.reshape(n_exp * cap_rows, d_model), flat_slot, axis=0, mode='fill', fill_value=0)
    return jnp.sum(rows, axis=1, dtype=jnp.float32).astype(jnp.bfloat16)


def expert_backward(x_rows, dz_rows, w_gate, w_down, w_up):
    a_pre = jnp.einsum('erd,edf->erf', x_rows, w_gate, preferred_element_type=jnp.float32).astype(jnp.bfloat16).astype(jnp.float32)
    b_pre = jnp.einsum('erd,edf->erf', x_rows, w_up, preferred_element_type=jnp.float32).astype(jnp.bfloat16).astype(jnp.float32)
    sigma_a = jax.nn.sigmoid(a_pre)
    silu_a = a_pre * sigma_a
    hidden = (silu_a * b_pre).astype(jnp.bfloat16)
    d_hidden = jnp.einsum('erd,efd->erf', dz_rows, w_down, preferred_element_type=jnp.float32)
    d_gate = (d_hidden * b_pre * sigma_a * (1.0 + a_pre * (1.0 - sigma_a))).astype(jnp.bfloat16)
    d_up = (d_hidden * silu_a).astype(jnp.bfloat16)
    g_down = jnp.einsum('erf,erd->efd', hidden, dz_rows, preferred_element_type=jnp.float32)
    g_gate = jnp.einsum('erd,erf->edf', x_rows, d_gate, preferred_element_type=jnp.float32)
    g_up = jnp.einsum('erd,erf->edf', x_rows, d_up, preferred_element_type=jnp.float32)
    dx_rows = (jnp.einsum('erf,edf->erd', d_gate, w_gate, preferred_element_type=jnp.float32) + jnp.einsum('erf,edf->erd', d_up, w_up, preferred_element_type=jnp.float32)).astype(jnp.bfloat16)
    return dx_rows, g_gate, g_down, g_up


def solution(mesh):
    n_dev = mesh.shape['ep']

    def local_step(x_loc, dy_loc, ids_loc, gate_loc, slot_loc, w_gate, w_down, w_up):
        tok_dev, top_k = ids_loc.shape
        n_local = w_gate.shape[0]
        n_exp = n_local * n_dev
        d_model = x_loc.shape[1]
        cap_rows = slot_capacity(tok_dev, top_k, n_exp)
        x_send, dz_send, flat_slot = source_dispatch(x_loc, dy_loc, ids_loc, gate_loc, slot_loc, cap_rows, n_exp)
        x_recv = lax.all_to_all(x_send.reshape(n_exp, 1, cap_rows, d_model), 'ep', 0, 1, tiled=True)
        dz_recv = lax.all_to_all(dz_send.reshape(n_exp, 1, cap_rows, d_model), 'ep', 0, 1, tiled=True)
        dx_rows, g_gate, g_down, g_up = expert_backward(x_recv.reshape(n_local, n_dev * cap_rows, d_model), dz_recv.reshape(n_local, n_dev * cap_rows, d_model), w_gate, w_down, w_up)
        dx_back = lax.all_to_all(dx_rows.reshape(n_local, n_dev, cap_rows, d_model), 'ep', 1, 0, tiled=True)
        dx_loc = source_combine(dx_back.reshape(n_exp, cap_rows, d_model), flat_slot)
        return dx_loc, g_gate, g_down, g_up

    tok_spec = P(('dp', 'ep'), None)
    w_spec = P('ep', None, None)
    grad_spec = P(('dp', 'ep'), None, None)
    return jax.shard_map(local_step, mesh=mesh, in_specs=(tok_spec, tok_spec, tok_spec, tok_spec, tok_spec, w_spec, w_spec, w_spec), out_specs=(tok_spec, grad_spec, grad_spec, grad_spec), check_vma=False)
```

profile of v0, /device:TPU:0, one launch (start us, length us, event | category | flops | bytes accessed | tf_op | source)
XLA Modules:
  0.0 111.7 jit_solution(7953063712456270514)
XLA Ops:
  0.6 0.7 compare_and_fusion.1
  1.5 0.1 reshape.71
  1.6 2.4 %scatter_custom_fusion = s32[768]{0:T(1024)S(1)} fusion(s32[512]{0:T(512)S(1)} %bitcast.54, s32[512]{0:T(512)S(1)} %iota.3, s32[]{:T(128)} %constant.58.clone.1), kind=kCustom, calls=%fused_computation.45 | custom fusion | bytes 3076 | tf_op jit(solution)/shard_map/scatter | solution.py:16
  4.1 2.8 %gather_fusion.3 = bf16[768,1024]{1,0:T(8,128)(2,1)S(1)} fusion(bf16[64,1024]{1,0:T(8,128)(2,1)S(1)} %copy-done, s32[1024]{0:T(1024)S(1)} %pad_clamp_fusion.1), kind=kCustom, calls=%fused_computation.1.clone | custom fusion | bytes 3148800 | tf_op jit(solution)/shard_map/jit(_take)/gather | solution.py:18
  6.9 1.3 %broadcast_select_fusion = bf16[768,1024]{1,0:T(8,128)(2,1)} fusion(bf16[768,1024]{1,0:T(8,128)(2,1)S(1)} %gather_fusion.3, pred[768]{0:T(1024)(128)(4,1)S(1)} %get-tuple-element.7), kind=kLoop, calls=%fused_computation.21 | loop fusion | flops 786432 | bytes 3146496 | tf_op jit(solution)/shard_map/jit(_take)/select_n | solution.py:18
  8.2 4.7 %all-to-all-start.1 = ((bf16[32,1,24,1024]{3,2,1,0:T(8,128)(2,1)}), bf16[32,1,24,1024]{3,2,1,0:T(8,128)(2,1)S(1)}, u32[]{:S(2)}, u32[]{:S(2)}) async-start(bf16[32,1,24,1024]{3,2,1,0:T(8,128)(2,1)} %bitcast.7), calls=%async_computation.1 | async-start | bytes 3145728 | tf_op jit(solution)/shard_map/all_to_all | solution.py:57
  13.0 0.1 copy.21
  13.1 0.1 copy.29
  13.2 0.1 reshape.102
  13.4 0.1 reshape.72
  13.5 3.6 %gather_fusion.2 = bf16[768,1024]{1,0:T(8,128)(2,1)} fusion(bf16[64,1024]{1,0:T(8,128)(2,1)S(1)} %copy-done.2, s32[1024]{0:T(1024)S(1)} %pad_clamp_fusion.1), kind=kCustom, calls=%fused_computation.clone | custom fusion | bytes 3148800 | tf_op jit(solution)/shard_map/jit(_take)/gather | solution.py:19
  17.0 5.0 %gather_fusion = f32[768]{0:T(1024)S(1)} fusion(f32[512]{0:T(512)S(1)} %reshape.72, s32[1024]{0:T(1024)S(1)} %pad_clamp_fusion.2), kind=kCustom, calls=%fused_computation.2 | custom fusion | bytes 9216 | tf_op jit(solution)/shard_map/jit(_take)/gather | solution.py:20
  22.1 3.0 %multiply_convert_fusion = bf16[768,1024]{1,0:T(8,128)(2,1)} fusion(bf16[768,1024]{1,0:T(8,128)(2,1)} %gather_fusion.2, f32[768]{0:T(1024)S(1)} %and_select_fusion, pred[768]{0:T(1024)(128)(4,1)S(1)} %get-tuple-element.7), kind=kLoop, calls=%fused_computation.6 | loop fusion | flops 3145728 | bytes 3149568 | tf_op jit(solution)/shard_map/convert_element_type | solution.py:21
  25.1 7.7 %all-to-all-done.1 = bf16[32,1,24,1024]{3,2,1,0:T(8,128)(2,1)S(1)} async-done(((bf16[32,1,24,1024]{3,2,1,0:T(8,128)(2,1)}), bf16[32,1,24,1024]{3,2,1,0:T(8,128)(2,1)S(1)}, u32[]{:S(2)}, u32[]{:S(2)}) %all-to-all-start.1) | async-done | bytes 1572896 | tf_op jit(solution)/shard_map/all_to_all | solution.py:57
  32.8 4.5 %all-to-all-start = ((bf16[32,1,24,1024]{3,2,1,0:T(8,128)(2,1)}), bf16[32,1,24,1024]{3,2,1,0:T(8,128)(2,1)}, u32[]{:S(2)}, u32[]{:S(2)}) async-start(bf16[32,1,24,1024]{3,2,1,0:T(8,128)(2,1)} %bitcast.2), calls=%async_computation | async-start | bytes 3145728 | tf_op jit(solution)/shard_map/all_to_all | solution.py:58
  37.4 0.2 copy.27
  37.5 5.0 %convolution_convert_fusion = bf16[8,96,512]{2,1,0:T(8,128)(2,1)S(1)} fusion(bf16[8,96,1024]{2,1,0:T(8,128)(2,1)S(1)} %bitcast.40, bf16[8,1024,512]{2,1,0:T(8,128)(2,1)} %param.15), kind=kOutput, calls=%fused_computation.22 | convolution fusion | flops 805699584 | bytes 10747904 | tf_op jit(solution)/shard_map/erd,edf->erf/dot_general | solution.py:32
  42.5 0.7 slice-done.3
  43.3 1.4 %convolution_convert_fusion.1 = bf16[8,96,512]{2,1,0:T(8,128)(2,1)S(1)} fusion(bf16[8,96,1024]{2,1,0:T(8,128)(2,1)S(1)} %bitcast.41, bf16[8,1024,512]{2,1,0:T(8,128)(2,1)S(1)} %bitcast.47), kind=kOutput, calls=%fused_computation.23 | convolution fusion | flops 805699584 | bytes 10747904 | tf_op jit(solution)/shard_map/erd,edf->erf/dot_general | solution.py:33
  44.7 12.3 %all-to-all-done = bf16[32,1,24,1024]{3,2,1,0:T(8,128)(2,1)} async-done(((bf16[32,1,24,1024]{3,2,1,0:T(8,128)(2,1)}), bf16[32,1,24,1024]{3,2,1,0:T(8,128)(2,1)}, u32[]{:S(2)}, u32[]{:S(2)}) %all-to-all-start) | async-done | bytes 1572896 | tf_op jit(solution)/shard_map/all_to_all | solution.py:58
  57.0 1.7 %copy.25 = bf16[8,4,1,24,1024]{4,3,1,0,2:T(8,128)(2,1)S(1)} copy(bf16[8,4,1,24,1024]{4,3,0,1,2:T(8,128)(2,1)} %bitcast.4) | data formatting | bytes 3145728 | tf_op jit(solution)/shard_map/all_to_all | solution.py:58
  58.7 9.3 %fusion.9 = f32[8,512,1024]{2,1,0:T(8,128)} fusion(bf16[8,96,1024]{2,1,0:T(8,128)(2,1)S(1)} %bitcast.50, bf16[8,96,512]{2,1,0:T(8,128)(2,1)S(1)} %convolution_convert_fusion.1, bf16[8,96,512]{2,1,0:T(8,128)(2,1)S(1)} %convolution_convert_fusion), kind=kOutput, calls=%fused_computation.26 | convolution fusion | flops 808452096 | bytes 19922944 | tf_op jit(solution)/shard_map/erf,erd->efd/dot_general | solution.py:40
  68.1 7.7 %fusion.2 = (bf16[8,96,512]{2,1,0:T(8,128)(2,1)}, f32[8,96,512]{2,1,0:T(8,128)}) fusion(bf16[8,96,512]{2,1,0:T(8,128)(2,1)S(1)} %convolution_convert_fusion.1, bf16[8,96,512]{2,1,0:T(8,128)(2,1)S(1)} %convolution_convert_fusion, bf16[8,96,1024]{2,1,0:T(8,128)(2,1)S(1)} %bitcast.51, bf16[8,512,1024]{2,1,0:T(8,128)(2,1)} %param.16), kind=kOutput, calls=%fused_computation.14 | convolution fusion | flops 810024960 | bytes 13893632 | tf_op jit(solution)/shard_map/erd,efd->erf/dot_general | solution.py:37
  75.8 3.8 %fusion.17 = f32[8,96,1024]{2,1,0:T(8,128)S(1)} fusion(bf16[8,96,512]{2,1,0:T(8,128)(2,1)} %get-tuple-element.9, bf16[8,1024,512]{2,1,0:T(8,128)(2,1)S(1)} %bitcast.45), kind=kOutput, calls=%fused_computation.49 | convolution fusion | flops 805306368 | bytes 12320768 | tf_op jit(solution)/shard_map/erf,edf->erd/dot_general | solution.py:43
  79.6 4.2 %add_convert_fusion = bf16[8,96,1024]{2,1,0:T(8,128)(2,1)S(1)} fusion(f32[8,96,1024]{2,1,0:T(8,128)S(1)} %fusion.17, bf16[8,1024,512]{2,1,0:T(8,128)(2,1)S(1)} %bitcast.49, f32[8,96,512]{2,1,0:T(8,128)} %get-tuple-element.10, bf16[8,96,512]{2,1,0:T(8,128)(2,1)S(1)} %convolution_convert_fusion), kind=kOutput, calls=%fused_computation.5 | convolution fusion | flops 809631744 | bytes 15466496 | tf_op jit(solution)/shard_map/erf,edf->erd/dot_general | solution.py:43
  83.7 1.3 %copy.28 = bf16[8,4,24,1024]{3,2,0,1:T(8,128)(2,1)} copy(bf16[8,4,24,1024]{3,2,1,0:T(8,128)(2,1)S(1)} %bitcast.53) | data formatting | bytes 3145728 | tf_op jit(solution)/shard_map/reshape | solution.py:60
  85.0 3.8 %all-to-all-start.2 = ((bf16[8,4,24,1024]{3,2,0,1:T(8,128)(2,1)}), bf16[8,4,24,1024]{3,2,0,1:T(8,128)(2,1)S(1)}, u32[]{:S(2)}, u32[]{:S(2)}) async-start(bf16[8,4,24,1024]{3,2,0,1:T(8,128)(2,1)} %copy.28), calls=%async_computation.2 | async-start | bytes 3145728 | tf_op jit(solution)/shard_map/all_to_all | solution.py:60
  88.9 9.8 %fusion.18 = f32[8,1024,512]{2,1,0:T(8,128)} fusion(bf16[8,96,1024]{2,1,0:T(8,128)(2,1)S(1)} %bitcast.42, bf16[8,96,512]{2,1,0:T(8,128)(2,1)} %get-tuple-element.9), kind=kOutput, calls=%fused_computation.50 | convolution fusion | flops 805306368 | bytes 19136512 | tf_op jit(solution)/shard_map/erd,erf->edf/dot_general | solution.py:41
  98.7 8.6 %fusion.16 = f32[8,1024,512]{2,1,0:T(8,128)} fusion(bf16[8,96,1024]{2,1,0:T(8,128)(2,1)S(1)} %bitcast.43, f32[8,96,512]{2,1,0:T(8,128)S(1)} %copy-done.5, bf16[8,96,512]{2,1,0:T(8,128)(2,1)S(1)} %copy-done.4), kind=kOutput, calls=%fused_computation.48 | convolution fusion | flops 808058880 | bytes 20709376 | tf_op jit(solution)/shard_map/erd,erf->edf/dot_general | solution.py:42
  107.3 1.2 %all-to-all-done.2 = bf16[8,4,24,1024]{3,2,0,1:T(8,128)(2,1)S(1)} async-done(((bf16[8,4,24,1024]{3,2,0,1:T(8,128)(2,1)}), bf16[8,4,24,1024]{3,2,0,1:T(8,128)(2,1)S(1)}, u32[]{:S(2)}, u32[]{:S(2)}) %all-to-all-start.2) | async-done | bytes 1572896 | tf_op jit(solution)/shard_map/all_to_all | solution.py:60
  108.4 2.0 %gather_fusion.1 = bf16[512,1024]{1,0:T(8,128)(2,1)S(1)} fusion(bf16[768,1024]{1,0:T(8,128)(2,1)S(1)} %bitcast.39, s32[1024]{0:T(1024)S(1)} %pad_clamp_fusion), kind=kCustom, calls=%fused_computation.3 | custom fusion | bytes 2099200 | tf_op jit(solution)/shard_map/jit(_take)/gather | solution.py:27
  110.5 1.2 %fusion.8 = bf16[64,1024]{1,0:T(8,128)(2,1)} fusion(bf16[512,1024]{1,0:T(8,128)(2,1)S(1)} %gather_fusion.1, pred[64,8]{1,0:T(8,128)(4,1)S(1)} %copy.21), kind=kLoop, calls=%fused_computation.25 | loop fusion | flops 983040 | bytes 1180160 | tf_op jit(solution)/shard_map/reduce_sum | solution.py:28
  (39 shorter events, 0.3 us)
Async XLA Ops:
  0.6 3.5 %copy-start = (bf16[64,1024]{1,0:T(8,128)(2,1)S(1)}, bf16[64,1024]{1,0:T(8,128)(2,1)}, u32[]{:S(2)}) copy-start(bf16[64,1024]{1,0:T(8,128)(2,1)} %param.10) | copy-start | bytes 393220
  8.2 5.0 %copy-start.6 = (f32[64,8]{0,1:T(8,128)S(1)}, f32[64,8]{0,1:T(8,128)}, u32[]{:S(2)}) copy-start(f32[64,8]{0,1:T(8,128)} %param.13) | copy-start | bytes 6148
  8.2 5.2 %copy-start.2 = (bf16[64,1024]{1,0:T(8,128)(2,1)S(1)}, bf16[64,1024]{1,0:T(8,128)(2,1)}, u32[]{:S(2)}) copy-start(bf16[64,1024]{1,0:T(8,128)(2,1)} %param.11) | copy-start | bytes 393220
  8.2 24.6 %all-to-all-start.1 = ((bf16[32,1,24,1024]{3,2,1,0:T(8,128)(2,1)}), bf16[32,1,24,1024]{3,2,1,0:T(8,128)(2,1)S(1)}, u32[]{:S(2)}, u32[]{:S(2)}) async-start(bf16[32,1,24,1024]{3,2,1,0:T(8,128)(2,1)} %bitcast.7), calls=%async_computation.1 | async-start | bytes 3145728 | tf_op jit(solution)/shard_map/all_to_all | solution.py:57
  32.8 24.1 %all-to-all-start = ((bf16[32,1,24,1024]{3,2,1,0:T(8,128)(2,1)}), bf16[32,1,24,1024]{3,2,1,0:T(8,128)(2,1)}, u32[]{:S(2)}, u32[]{:S(2)}) async-start(bf16[32,1,24,1024]{3,2,1,0:T(8,128)(2,1)} %bitcast.2), calls=%async_computation | async-start | bytes 3145728 | tf_op jit(solution)/shard_map/all_to_all | solution.py:58
  37.4 5.2 %slice-start.2 = ((s8[8388608]{0:T(1024)(128)(4,1)}), s8[4194304]{0:T(1024)(128)(4,1)S(1)}, s32[]{:S(2)}) async-start(s8[8388608]{0:T(1024)(128)(4,1)} %bitcast.46), calls=%async_computation.5 | async-start | bytes 8388608
  37.5 5.7 %slice-start.3 = ((s8[8388608]{0:T(1024)(128)(4,1)}), s8[4194304]{0:T(1024)(128)(4,1)S(1)}, s32[]{:S(2)}) async-start(s8[8388608]{0:T(1024)(128)(4,1)} %bitcast.46), calls=%async_computation.6 | async-start | bytes 8388608
  43.3 36.3 %copy-start.3 = (bf16[8,96,512]{2,1,0:T(8,128)(2,1)}, bf16[8,96,512]{2,1,0:T(8,128)(2,1)S(1)}, u32[]{:S(2)}) copy-start(bf16[8,96,512]{2,1,0:T(8,128)(2,1)S(1)} %convolution_convert_fusion) | copy-start | bytes 2359300
  57.0 18.8 %slice-start = ((s8[8388608]{0:T(1024)(128)(4,1)}), s8[4194304]{0:T(1024)(128)(4,1)S(1)}, s32[]{:S(2)}) async-start(s8[8388608]{0:T(1024)(128)(4,1)} %bitcast.44), calls=%async_computation.3 | async-start | bytes 8388608
  57.0 22.6 %slice-start.4 = ((s8[8388608]{0:T(1024)(128)(4,1)}), s8[4194304]{0:T(1024)(128)(4,1)S(1)}, s32[]{:S(2)}) async-start(s8[8388608]{0:T(1024)(128)(4,1)} %bitcast.48), calls=%async_computation.7 | async-start | bytes 8388608
  58.7 17.1 %slice-start.1 = ((s8[8388608]{0:T(1024)(128)(4,1)}), s8[4194304]{0:T(1024)(128)(4,1)S(1)}, s32[]{:S(2)}) async-start(s8[8388608]{0:T(1024)(128)(4,1)} %bitcast.44), calls=%async_computation.4 | async-start | bytes 8388608
  58.7 20.9 %slice-start.5 = ((s8[8388608]{0:T(1024)(128)(4,1)}), s8[4194304]{0:T(1024)(128)(4,1)S(1)}, s32[]{:S(2)}) async-start(s8[8388608]{0:T(1024)(128)(4,1)} %bitcast.48), calls=%async_computation.8 | async-start | bytes 8388608
  85.0 23.4 %all-to-all-start.2 = ((bf16[8,4,24,1024]{3,2,0,1:T(8,128)(2,1)}), bf16[8,4,24,1024]{3,2,0,1:T(8,128)(2,1)S(1)}, u32[]{:S(2)}, u32[]{:S(2)}) async-start(bf16[8,4,24,1024]{3,2,0,1:T(8,128)(2,1)} %copy.28), calls=%async_computation.2 | async-start | bytes 3145728 | tf_op jit(solution)/shard_map/all_to_all | solution.py:60
  88.8 9.9 %copy-start.4 = (bf16[8,96,512]{2,1,0:T(8,128)(2,1)S(1)}, bf16[8,96,512]{2,1,0:T(8,128)(2,1)}, u32[]{:S(2)}) copy-start(bf16[8,96,512]{2,1,0:T(8,128)(2,1)} %copy-done.3) | copy-start | bytes 2359300
  88.8 9.9 %copy-start.5 = (f32[8,96,512]{2,1,0:T(8,128)S(1)}, f32[8,96,512]{2,1,0:T(8,128)}, u32[]{:S(2)}) copy-start(f32[8,96,512]{2,1,0:T(8,128)} %get-tuple-element.10) | copy-start | bytes 4718596
  108.4 3.3 %copy-start.1 = (bf16[64,1024]{1,0:T(8,128)(2,1)S(1)}, bf16[64,1024]{1,0:T(8,128)(2,1)}, u32[]{:S(2)}) copy-start(bf16[64,1024]{1,0:T(8,128)(2,1)} %param.10) | copy-start | bytes 393220
where the time goes:
time: 112 us
  matrix products  49.8 us (44%)
  waiting for transfers between devices  21.2 us (19%)
  local copies, waits for them, and re-layouts  20.5 us (18%)
  starting transfers between devices  13.1 us (12%)
  other arithmetic  6.35 us (6%)
    all_to_all x1, waiting for transfers between devices, local_step(): lax.all_to_all(dz_send.reshape(n_exp, 1, cap_rows, d_model), 'ep', 0, 1,...  12.3 us
    dot_general x1, matrix products, expert_backward(): jnp.einsum('erd,erf->edf', x_rows, d_gate, preferred_element_type=jnp.flo...  9.84 us
    dot_general x1, matrix products, expert_backward(): jnp.einsum('erf,erd->efd', hidden, dz_rows, preferred_element_type=jnp.fl...  9.35 us
    dot_general x1, matrix products, expert_backward(): jnp.einsum('erd,erf->edf', x_rows, d_up, preferred_element_type=jnp.float32)  8.55 us
    all_to_all x1, waiting for transfers between devices, local_step(): lax.all_to_all(x_send.reshape(n_exp, 1, cap_rows, d_model), 'ep', 0, 1, t...  7.75 us
    dot_general x1, matrix products, expert_backward(): jnp.einsum('erd,efd->erf', dz_rows, w_down, preferred_element_type=jnp.fl...  7.69 us
    gather x1, local copies, waits for them, and re-layouts, source_dispatch(): jnp.take(gate_src.reshape(n_copy), slot_copy, mode='fill', fill_value=0)  5.01 us
    dot_general x1, matrix products, expert_backward(): jnp.einsum('erd,edf->erf', x_rows, w_gate, preferred_element_type=jnp.flo...  4.97 us
  transfers between devices with their start and end apart: 3, of which 3 were waited for; matrix products, arithmetic and copies ran while one was open for 33% of the time, Pallas kernels for 0%

commit v1 on v0

v1 whole, which is shorter than its diff:
```python
import functools

import jax
import jax.numpy as jnp
from jax import lax
from jax.experimental import pallas as pl
from jax.experimental.pallas import tpu as pltpu
from jax.sharding import PartitionSpec as P

MESH = pl.DeviceIdType.MESH
F32 = jnp.float32
BF16 = jnp.bfloat16
NN = (((1,), (0,)), ((), ()))
NT = (((1,), (1,)), ((), ()))
TN = (((0,), (0,)), ((), ()))


def slot_capacity(tok_dev, top_k, n_exp):
    return ((3 * tok_dev * top_k) // (2 * n_exp) + 7) // 8 * 8


def mm(a, b, dims):
    return lax.dot_general(a, b, dims, preferred_element_type=F32)


def peers():
    ep = lax.axis_index('ep')
    core = lax.rem(ep, 2)
    chip = ep - core
    mate = chip + 1 - core
    far = lax.rem(ep + 2, 4)
    far_mate = lax.rem(mate + 2, 4)
    return ep, mate, far, far_mate


def entry_barrier(others):
    barrier = pltpu.get_barrier_semaphore()
    for other in others:
        pl.semaphore_signal(barrier, inc=1, device_id={'ep': other}, device_id_type=MESH)
    pl.semaphore_wait(barrier, len(others))


def gather_kernel(cap, x_hbm, dy_hbm, ids_hbm, slot_hbm, gate_hbm, w1_hbm, w3_hbm, w2_hbm, xg, dyg, metag, w1, w3, w2, x_ref, dy_ref, ids_ref, slot_ref, gate_ref, meta, w_sem, loc_sem, send_sem, recv_sem):
    ep, mate, far, far_mate = peers()
    n_local = w1.shape[0]
    tok = x_ref.shape[0]
    small = []
    for k, (src, dst) in enumerate(((x_hbm, x_ref), (dy_hbm, dy_ref), (ids_hbm, ids_ref), (slot_hbm, slot_ref), (gate_hbm, gate_ref))):
        c = pltpu.make_async_copy(src, dst, loc_sem.at[k])
        c.start()
        small.append(c)
    copies = []
    for e in range(n_local):
        for k, (src, dst) in enumerate(((w1_hbm, w1), (w3_hbm, w3), (w2_hbm, w2))):
            c = pltpu.make_async_copy(src.at[e], dst.at[e], w_sem.at[k, e])
            c.start()
            copies.append(c)
    meta[...] = jnp.zeros_like(meta)
    for c in small:
        c.wait()
    key = jnp.where(slot_ref[...] >= 0, ids_ref[...] * cap + slot_ref[...], -1)
    meta[0:8, 0:tok] = key.astype(F32)
    meta[8:16, 0:tok] = gate_ref[...]
    entry_barrier((mate, far, far_mate))
    remote = []

    def send(src, dst, k, to):
        c = pltpu.make_async_remote_copy(src_ref=src, dst_ref=dst, send_sem=send_sem.at[k], recv_sem=recv_sem.at[k], device_id={'ep': to}, device_id_type=MESH)
        c.start()
        remote.append(c)
        return c

    half = tok // 2
    mine = pl.multiple_of(ep * tok, tok)
    pieces = [(src, dst, h * half) for src, dst in ((x_ref, xg), (dy_ref, dyg)) for h in range(2)]
    from_far = []
    for k, (src, dst, off) in enumerate(pieces):
        from_far.append(send(src.at[pl.ds(off, half)], dst.at[pl.ds(mine + off, half)], k, far))
    for k, (src, dst, off) in enumerate(pieces):
        send(src.at[pl.ds(off, half)], dst.at[pl.ds(mine + off, half)], 4 + k, mate)
    for k, to in enumerate((far, mate, far_mate)):
        send(meta, metag.at[ep], 12 + k, to)
    xg[pl.ds(mine, tok), :] = x_ref[...]
    dyg[pl.ds(mine, tok), :] = dy_ref[...]
    metag[ep] = meta[...]
    theirs = pl.multiple_of(far * tok, tok)
    for k, (src, dst, off) in enumerate(pieces):
        from_far[k].wait_recv()
        here = dst.at[pl.ds(theirs + off, half)]
        send(here, here, 8 + k, mate)
    for c in from_far:
        c.wait_send()
    for c in remote[4:]:
        c.wait()
    for c in copies:
        c.wait()


def expert_kernel(cap, n_src, xg, dyg, metag, w1, w3, w2, g1, g3, g2, part, p_all, x_all, dz_all, dx_all, s1, s3, s2, out_sem):
    ep = lax.axis_index('ep')
    n_local = w1.shape[0]
    rows = n_src * cap
    n_tok = xg.shape[0]
    tok = n_tok // n_src
    halves = []
    for pair in range(n_src // 2):
        halves.append(metag[2 * pair] + pltpu.roll(metag[2 * pair + 1], tok, 1))
    meta = jnp.concatenate(halves, axis=1)
    key = meta[0:8, :].astype(jnp.int32)
    gate = meta[8:16, :]
    lane = lax.broadcasted_iota(jnp.int32, (1, n_tok), 1)
    src_base = (lane // tok) * cap
    row_id = lax.broadcasted_iota(jnp.int32, (rows, n_tok), 0)

    def dispatch(e):
        lo = (ep * n_local + e) * cap
        hit = (key >= lo) & (key < lo + cap)
        slot = jnp.sum(jnp.where(hit, key - lo + 1, 0), axis=0, keepdims=True)
        g_tok = jnp.sum(jnp.where(hit, gate, 0.0), axis=0, keepdims=True)
        want = jnp.where(slot > 0, slot - 1 + src_base, -1)
        pick = row_id == want
        g_row = jnp.sum(jnp.where(pick, g_tok, 0.0), axis=1, keepdims=True)
        sel = jnp.where(pick, 1.0, 0.0).astype(BF16)
        p_all[e] = sel
        x_rows = mm(sel, xg[...], NN).astype(BF16)
        dy_rows = mm(sel, dyg[...], NN)
        x_all[e] = x_rows
        dz_all[e] = (g_row * dy_rows).astype(BF16)

    def copies(e, slot):
        return [pltpu.make_async_copy(s.at[slot], g.at[e], out_sem.at[k, slot]) for k, (s, g) in enumerate(((s1, g1), (s3, g3), (s2, g2)))]

    def step(e, carry):
        slot = lax.rem(e, 2)

        @pl.when(e >= 2)
        def _():
            for c in copies(e - 2, slot):
                c.wait()

        dispatch(e)
        x_rows = x_all[e]
        dz_rows = dz_all[e]
        a = mm(x_rows, w1[e], NN).astype(BF16).astype(F32)
        b = mm(x_rows, w3[e], NN).astype(BF16).astype(F32)
        dh = mm(dz_rows, w2[e], NT)
        sg = jax.nn.sigmoid(a)
        silu = a * sg
        h = (silu * b).astype(BF16)
        da = (dh * b * sg * (1.0 + a * (1.0 - sg))).astype(BF16)
        db = (dh * silu).astype(BF16)
        dx_all[e] = (mm(da, w1[e], NT) + mm(db, w3[e], NT)).astype(BF16)
        s2[slot] = mm(h, dz_rows, TN)
        s1[slot] = mm(x_rows, da, TN)
        s3[slot] = mm(x_rows, db, TN)
        for c in copies(e, slot):
            c.start()
        return carry

    lax.fori_loop(0, n_local, step, 0)
    total = mm(p_all[...].reshape(n_local * rows, n_tok), dx_all[...].reshape(n_local * rows, -1), TN)
    for s in range(n_src):
        part[s] = total[s * tok:(s + 1) * tok]
    for e in (n_local - 2, n_local - 1):
        for c in copies(e, e % 2):
            c.wait()


def reduce_kernel(part, dx_ref, got, pair, far_got, send_sem, recv_sem):
    ep, mate, far, far_mate = peers()
    entry_barrier((mate, far))
    tok = part.shape[1]
    n_chunk = 4
    q = tok // n_chunk

    def send(src, dst, k, to):
        c = pltpu.make_async_remote_copy(src_ref=src, dst_ref=dst, send_sem=send_sem.at[k], recv_sem=recv_sem.at[k], device_id={'ep': to}, device_id_type=MESH)
        c.start()
        return c

    first = []
    for i in range(n_chunk):
        first.append(send(part.at[far_mate, pl.ds(i * q, q)], got.at[0, pl.ds(i * q, q)], i, mate))
    last = send(part.at[mate], got.at[1], n_chunk, mate)
    hops = []
    for i in range(n_chunk):
        first[i].wait_recv()
        rows = pl.ds(i * q, q)
        pair[rows, :] = part[far, rows, :] + got[0, rows, :]
        if i > 0:
            rows = pl.ds((i - 1) * q, q)
            hops.append(send(pair.at[rows], far_got.at[rows], n_chunk + i, far))
    last.wait_recv()
    mine = part[ep] + got[1]
    rows = pl.ds((n_chunk - 1) * q, q)
    hops.append(send(pair.at[rows], far_got.at[rows], 2 * n_chunk, far))
    for i in range(n_chunk):
        hops[i].wait_recv()
        dx_ref[i * q:(i + 1) * q, :] = (mine[i * q:(i + 1) * q, :] + far_got[i * q:(i + 1) * q, :]).astype(BF16)
    for c in first + [last] + hops:
        c.wait_send()


def solution(mesh):
    n_src = mesh.shape['ep']
    vmem = pl.BlockSpec(memory_space=pltpu.VMEM)
    hbm = pl.BlockSpec(memory_space=pltpu.HBM)

    def local_step(x_loc, dy_loc, ids_loc, gate_loc, slot_loc, w_gate, w_down, w_up):
        tok, top_k = ids_loc.shape
        n_local, d_model, ff = w_gate.shape
        n_exp = n_local * n_src
        cap = slot_capacity(tok, top_k, n_exp)
        rows = n_src * cap
        n_tok = n_src * tok
        dma = pltpu.SemaphoreType.DMA
        xg, dyg, metag, w1, w3, w2 = pl.pallas_call(
            functools.partial(gather_kernel, cap),
            out_shape=(
                pltpu.VMEM((n_tok, d_model), BF16),
                pltpu.VMEM((n_tok, d_model), BF16),
                pltpu.VMEM((n_src, 16, 128), F32),
                pltpu.VMEM(w_gate.shape, BF16),
                pltpu.VMEM(w_up.shape, BF16),
                pltpu.VMEM(w_down.shape, BF16),
            ),
            in_specs=[hbm] * 8,
            out_specs=(vmem,) * 6,
            scratch_shapes=[
                pltpu.VMEM((tok, d_model), BF16),
                pltpu.VMEM((tok, d_model), BF16),
                pltpu.VMEM((top_k, tok), jnp.int32),
                pltpu.VMEM((top_k, tok), jnp.int32),
                pltpu.VMEM((top_k, tok), F32),
                pltpu.VMEM((16, 128), F32),
                dma((3, n_local)),
                dma((5,)),
                dma((15,)),
                dma((15,)),
            ],
            compiler_params=pltpu.CompilerParams(collective_id=0, has_side_effects=True, vmem_limit_bytes=4 << 20),
            name='gather',
        )(*(pltpu.with_memory_space_constraint(v, pltpu.HBM) for v in (x_loc, dy_loc, ids_loc.T, slot_loc.T, gate_loc.T, w_gate, w_up, w_down)))
        g1, g3, g2, part = pl.pallas_call(
            functools.partial(expert_kernel, cap, n_src),
            out_shape=(
                pltpu.HBM((n_local, d_model, ff), F32),
                pltpu.HBM((n_local, d_model, ff), F32),
                pltpu.HBM((n_local, ff, d_model), F32),
                pltpu.VMEM((n_src, tok, d_model), F32),
            ),
            in_specs=[vmem] * 6,
            out_specs=(hbm, hbm, hbm, vmem),
            scratch_shapes=[
                pltpu.VMEM((n_local, rows, n_tok), BF16),
                pltpu.VMEM((n_local, rows, d_model), BF16),
                pltpu.VMEM((n_local, rows, d_model), BF16),
                pltpu.VMEM((n_local, rows, d_model), BF16),
                pltpu.VMEM((2, d_model, ff), F32),
                pltpu.VMEM((2, d_model, ff), F32),
                pltpu.VMEM((2, ff, d_model), F32),
                dma((3, 2)),
            ],
            compiler_params=pltpu.CompilerParams(vmem_limit_bytes=24 << 20),
            name='experts',
        )(xg, dyg, metag, w1, w3, w2)
        dx_loc = pl.pallas_call(
            reduce_kernel,
            out_shape=jax.ShapeDtypeStruct((tok, d_model), BF16),
            in_specs=[vmem],
            out_specs=vmem,
            scratch_shapes=[
                pltpu.VMEM((2, tok, d_model), F32),
                pltpu.VMEM((tok, d_model), F32),
                pltpu.VMEM((tok, d_model), F32),
                dma((9,)),
                dma((9,)),
            ],
            compiler_params=pltpu.CompilerParams(collective_id=1, has_side_effects=True, vmem_limit_bytes=4 << 20),
            name='reduce',
        )(part)
        return dx_loc, g1, g2, g3

    tok_spec = P(('dp', 'ep'), None)
    w_spec = P('ep', None, None)
    grad_spec = P(('dp', 'ep'), None, None)
    return jax.shard_map(local_step, mesh=mesh, in_specs=(tok_spec, tok_spec, tok_spec, tok_spec, tok_spec, w_spec, w_spec, w_spec), out_specs=(tok_spec, grad_spec, grad_spec, grad_spec), check_vma=False)
```

time: 112 us -> 53.7 us (0.48)
  Pallas kernels: 0 us -> 52.3 us
  matrix products: 49.8 us -> 0 us
  waiting for transfers between devices: 21.2 us -> 0 us
  local copies, waits for them, and re-layouts: 20.5 us -> 0.66 us
  starting transfers between devices: 13.1 us -> 0 us
  other arithmetic: 6.35 us -> 0 us
    pallas_call x0 -> x3, Pallas kernels: none -> 52.3 us  [the longest x1 22.6 us: local_step(): pl.pallas_call(functools.partial(expert_kernel, cap, n_src), out_shape=(p...]
    dot_general x8 -> x0, matrix products: 49.8 us -> none  [the longest x1 9.84 us: expert_backward(): jnp.einsum('erd,erf->edf', x_rows, d_gate, preferred_element_type=jnp.flo...]
    all_to_all x3 -> x0, waiting for transfers between devices: 21.2 us -> none  [the longest x1 12.3 us: local_step(): lax.all_to_all(dz_send.reshape(n_exp, 1, cap_rows, d_model), 'ep', 0, 1,...]
    gather x4 -> x0, local copies, waits for them, and re-layouts: 13.4 us -> none  [the longest x1 5.01 us: source_dispatch(): jnp.take(gate_src.reshape(n_copy), slot_copy, mode='fill', fill_value=0)]
    all_to_all x3 -> x0, starting transfers between devices: 13.1 us -> none  [the longest x1 4.74 us: local_step(): lax.all_to_all(x_send.reshape(n_exp, 1, cap_rows, d_model), 'ep', 0, 1, t...]
    convert_element_type x1 -> x0, other arithmetic: 3 us -> none  [source_dispatch(): dz_send = (gate_slot[:, None] * dy_send).astype(jnp.bfloat16)]
    scatter x1 -> x0, local copies, waits for them, and re-layouts: 2.45 us -> none  [source_dispatch(): jnp.full((n_exp * cap_rows,), n_copy, jnp.int32)]
    all_to_all x2 -> x0, local copies, waits for them, and re-layouts: 1.86 us -> none  [the longest x1 1.7 us: local_step(): lax.all_to_all(dz_send.reshape(n_exp, 1, cap_rows, d_model), 'ep', 0, 1,...]
  transfers between devices with their start and end apart: 3 -> 0, of which waited for: 3 -> 0; matrix products, arithmetic and copies ran while one was open for 33% -> 0% of each run, Pallas kernels for 0% -> 0%
where the time goes in v1:
time: 53.7 us; the launch traced here: 53.6 us
  Pallas kernels  52.3 us (97%)
  local copies, waits for them, and re-layouts  0.66 us (1%)
  between operations  0.66 us (1%)
    pallas_call x1, Pallas kernels, local_step(): pl.pallas_call(functools.partial(expert_kernel, cap, n_src), out_shape=(p...  22.6 us
    pallas_call x1, Pallas kernels, local_step(): pl.pallas_call(functools.partial(gather_kernel, cap), out_shape=(pltpu.VM...  19.7 us
    pallas_call x1, Pallas kernels, local_step(): pl.pallas_call(reduce_kernel, out_shape=jax.ShapeDtypeStruct((tok, d_mode...  10 us

profile of v1, /device:TPU:0, one launch (start us, length us, event | category | flops | bytes accessed | tf_op | source)
XLA Modules:
  0.0 53.6 jit_solution(17443470301032404670)
XLA Ops:
  0.6 19.7 %gather.1 = (bf16[256,1024]{1,0:T(8,128)(2,1)S(1)}, bf16[256,1024]{1,0:T(8,128)(2,1)S(1)}, f32[4,16,128]{2,1,0:T(8,128)S(1)}, bf16[8,1024,512]{2,1,0:T(8,128)(2,...) custom-call(bf16[64,1024]{1,0:T(8,128)(2,1)} %x_hbm.1, bf16[64,1024]{1,0:T(8,128)(2,1)} %dy_hbm.1, ...), custom_call_target="tpu_custom_call" | custom-call | tf_op jit(solution)/shard_map/gather/pallas_call | solution.py:217
  20.3 22.6 %experts.1 = (f32[8,1024,512]{2,1,0:T(8,128)}, f32[8,1024,512]{2,1,0:T(8,128)}, f32[8,512,1024]{2,1,0:T(8,128)}, f32[4,64,1024]{2,1,0:T(8,128)S(1)}) custom-call(bf16[256,1024]{1,0:T(8,128)(2,1)S(1)} %get-tuple-element.14.xg, bf16[256,1024]{1,0:T(8,128)(2,1)S(1)} %get-tuple-element.15.dyg, f32[4,16,128]{2,1,0:T(8,128)S(1)} %get-tuple-element.16.metag, ...), custom_call_target="tpu_custom_call" | custom-call | tf_op jit(solution)/shard_map/experts/pallas_call | solution.py:244
  42.9 10.0 %reduce.1 = bf16[64,1024]{1,0:T(8,128)(2,1)S(1)} custom-call(f32[4,64,1024]{2,1,0:T(8,128)S(1)} %get-tuple-element.20.part), custom_call_target="tpu_custom_call" | custom-call | tf_op jit(solution)/shard_map/reduce/pallas_call | solution.py:267
  52.9 0.7 %copy.13 = bf16[64,1024]{1,0:T(8,128)(2,1)} copy(bf16[64,1024]{1,0:T(8,128)(2,1)S(1)} %reduce.1) | data formatting | bytes 262144

commit v2 on v0

v2 whole, which is shorter than its diff:
```python
import functools

import jax
import jax.numpy as jnp
from jax import lax
from jax.experimental import pallas as pl
from jax.experimental.pallas import tpu as pltpu
from jax.sharding import PartitionSpec as P

MESH = pl.DeviceIdType.MESH
F32 = jnp.float32
BF16 = jnp.bfloat16
NN = (((1,), (0,)), ((), ()))
NT = (((1,), (1,)), ((), ()))
TN = (((0,), (0,)), ((), ()))
N_FIRST = 5
N_BUF = 4
N_EARLY = 5
N_MID = 4


def slot_capacity(tok_dev, top_k, n_exp):
    return ((3 * tok_dev * top_k) // (2 * n_exp) + 7) // 8 * 8


def mm(a, b, dims):
    return lax.dot_general(a, b, dims, preferred_element_type=F32)


def peers():
    ep = lax.axis_index('ep')
    core = lax.rem(ep, 2)
    chip = ep - core
    mate = chip + 1 - core
    far = lax.rem(ep + 2, 4)
    far_mate = lax.rem(mate + 2, 4)
    return ep, mate, far, far_mate


def entry_barrier(others):
    barrier = pltpu.get_barrier_semaphore()
    for other in others:
        pl.semaphore_signal(barrier, inc=1, device_id={'ep': other}, device_id_type=MESH)
    pl.semaphore_wait(barrier, len(others))


def run(lo, hi, body, unroll):
    def step(e, carry):
        body(e)
        return carry

    if unroll == 0:
        for e in range(lo, hi):
            body(e)
    else:
        lax.fori_loop(lo, hi, step, 0, unroll=unroll)


def gather_kernel(cap, x_hbm, dy_hbm, ids_hbm, slot_hbm, gate_hbm, w1_hbm, w3_hbm, w2_hbm, dyg, metag, p_all, x_all, a_all, b_all, w1t, w3t, w2t, xg, ids_ref, slot_ref, gate_ref, w1, w3, w2, w_sem, loc_sem, send_sem, recv_sem):
    ep, mate, far, far_mate = peers()
    n_local, rows, n_tok = p_all.shape
    n_src = metag.shape[0]
    tok = n_tok // n_src
    barrier = pltpu.get_barrier_semaphore()
    for other in (mate, far, far_mate):
        pl.semaphore_signal(barrier, inc=1, device_id={'ep': other}, device_id_type=MESH)
    mine = pl.multiple_of(ep * tok, tok)
    theirs = pl.multiple_of(far * tok, tok)
    small = []
    for k, (src, dst) in enumerate(((x_hbm, xg.at[pl.ds(mine, tok)]), (dy_hbm, dyg.at[pl.ds(mine, tok)]), (ids_hbm, ids_ref), (slot_hbm, slot_ref), (gate_hbm, gate_ref))):
        c = pltpu.make_async_copy(src, dst, loc_sem.at[k])
        c.start()
        small.append(c)

    def loads(e):
        return [pltpu.make_async_copy(src.at[e], dst.at[e], w_sem.at[k, e]) for k, (src, dst) in enumerate(((w1_hbm, w1), (w3_hbm, w3), (w2_hbm, w2)))]

    for e in range(n_local):
        for c in loads(e):
            c.start(priority=1)
    for c in small:
        c.wait()
    key = jnp.where(slot_ref[...] >= 0, ids_ref[...] * cap + slot_ref[...], -1)
    metag[ep, 0:8, 0:tok] = key.astype(F32)
    metag[ep, 8:16, 0:tok] = gate_ref[...]
    metag[ep, 0:8, tok:2 * tok] = jnp.zeros((8, tok), F32)
    metag[ep, 8:16, tok:2 * tok] = jnp.zeros((8, tok), F32)
    pl.semaphore_wait(barrier, 3)

    def send(src, dst, k, to):
        c = pltpu.make_async_remote_copy(src_ref=src, dst_ref=dst, send_sem=send_sem.at[k], recv_sem=recv_sem.at[k], device_id={'ep': to}, device_id_type=MESH)
        c.start()
        return c

    half = tok // 2
    pieces = [(ref, h * half) for ref in (xg, dyg) for h in range(2)]

    def block(ref, base, off):
        return ref.at[pl.ds(base + off, half)]

    to_far = [send(block(ref, mine, off), block(ref, mine, off), k, far) for k, (ref, off) in enumerate(pieces)]
    to_mate = [send(block(ref, mine, off), block(ref, mine, off), 4 + k, mate) for k, (ref, off) in enumerate(pieces)]
    metas = [send(metag.at[ep], metag.at[ep], 12 + k, to) for k, to in enumerate((far, mate, far_mate))]
    r256 = lax.broadcasted_iota(jnp.int32, (256, 256), 0)
    c256 = lax.broadcasted_iota(jnp.int32, (256, 256), 1)
    eye = jnp.where(r256 == c256, 1.0, 0.0).astype(BF16)

    def turn(e):
        for c in loads(e):
            c.wait()
        w1t[e] = w1[e].T
        w3t[e] = w3[e].T
        for q in range(w2.shape[2] // 256):
            w2t[e, q * 256:(q + 1) * 256, :] = mm(eye, w2[e, :, q * 256:(q + 1) * 256], NT).astype(BF16)

    relays = []

    def relay(k):
        ref, off = pieces[k]
        to_far[k].wait_recv()
        relays.append(send(block(ref, theirs, off), block(ref, theirs, off), 8 + k, mate))

    run(0, N_EARLY, turn, 1)
    relay(0)
    relay(1)
    run(N_EARLY, n_local, turn, 1)
    for c in to_mate[:2] + relays[:2] + metas:
        c.wait_recv()
    lane = lax.broadcasted_iota(jnp.int32, (1, n_tok), 1)
    src_base = (lane // tok) * cap
    row_id = lax.broadcasted_iota(jnp.int32, (rows, n_tok), 0)
    key = all_meta(metag, tok)[0:8, :].astype(jnp.int32)

    def front(e):
        lo = (ep * n_local + e) * cap
        hit = (key >= lo) & (key < lo + cap)
        slot = jnp.sum(jnp.where(hit, key - lo + 1, 0), axis=0, keepdims=True)
        want = jnp.where(slot > 0, slot - 1 + src_base, -1)
        sel = jnp.where(row_id == want, 1.0, 0.0).astype(BF16)
        p_all[e] = sel
        x_rows = mm(sel, xg[...], NN).astype(BF16)
        x_all[e] = x_rows
        a_all[e] = mm(x_rows, w1[e], NN).astype(BF16)
        b_all[e] = mm(x_rows, w3[e], NN).astype(BF16)

    run(0, N_MID, front, 2)
    relay(2)
    relay(3)
    run(N_MID, n_local, front, 2)
    for c in to_mate[2:] + relays[2:]:
        c.wait_recv()
    for c in to_far + to_mate + relays + metas:
        c.wait_send()


def all_meta(metag, tok):
    halves = []
    for pair in range(metag.shape[0] // 2):
        halves.append(metag[2 * pair] + pltpu.roll(metag[2 * pair + 1], tok, 1))
    return jnp.concatenate(halves, axis=1)


def grad_copies(stage, grads, out_sem, e, slot):
    return [pltpu.make_async_copy(s.at[slot], g.at[e], out_sem.at[k, slot]) for k, (s, g) in enumerate(zip(stage, grads))]


def weight_grads(rows_in, stage, e, slot):
    x_all, dz_all, h_all, da_all, db_all = rows_in
    s1, s3, s2 = stage
    x_rows = x_all[e]
    s2[slot] = mm(h_all[e], dz_all[e], TN)
    s1[slot] = mm(x_rows, da_all[e], TN)
    s3[slot] = mm(x_rows, db_all[e], TN)


def expert_kernel(cap, n_first, dyg, metag, p_all, x_all, a_all, b_all, w1t, w3t, w2t, g1, g3, g2, part, dz_all, h_all, da_all, db_all, dx_all, s1, s3, s2, out_sem):
    ep = lax.axis_index('ep')
    n_local, rows, n_tok = p_all.shape
    n_src = metag.shape[0]
    tok = n_tok // n_src
    meta = all_meta(metag, tok)
    key = meta[0:8, :].astype(jnp.int32)
    gate = meta[8:16, :]
    rows_in = (x_all, dz_all, h_all, da_all, db_all)
    stage = (s1, s3, s2)
    grads = (g1, g3, g2)

    def middle(e):
        lo = (ep * n_local + e) * cap
        g_tok = jnp.sum(jnp.where((key >= lo) & (key < lo + cap), gate, 0.0), axis=0, keepdims=True)
        sel = p_all[e]
        g_row = jnp.sum(sel.astype(F32) * g_tok, axis=1, keepdims=True)
        dz_rows = (g_row * mm(sel, dyg[...], NN)).astype(BF16)
        dz_all[e] = dz_rows
        dh = mm(dz_rows, w2t[e], NN)
        a = a_all[e].astype(F32)
        b = b_all[e].astype(F32)
        sg = jax.nn.sigmoid(a)
        silu = a * sg
        h_all[e] = (silu * b).astype(BF16)
        da_all[e] = (dh * b * sg * (1.0 + a * (1.0 - sg))).astype(BF16)
        db_all[e] = (dh * silu).astype(BF16)

    def back(e):
        dx_all[e] = (mm(da_all[e], w1t[e], NN) + mm(db_all[e], w3t[e], NN)).astype(BF16)

    def first(e):
        middle(e)
        back(e)
        slot = lax.rem(e, 2)

        @pl.when(e >= 2)
        def _():
            for c in grad_copies(stage, grads, out_sem, e - 2, slot):
                c.wait()

        weight_grads(rows_in, stage, e, slot)
        for c in grad_copies(stage, grads, out_sem, e, slot):
            c.start()

    def later(e):
        middle(e)
        back(e)

    run(0, n_first, first, 1)
    run(n_first, n_local, later, 1)
    total = mm(p_all[...].reshape(n_local * rows, n_tok), dx_all[...].reshape(n_local * rows, -1), TN)
    for s in range(n_src):
        part[s] = total[s * tok:(s + 1) * tok]
    for e in range(max(n_first - 2, 0), n_first):
        for c in grad_copies(stage, grads, out_sem, e, e % 2):
            c.wait()


def rest_kernel(n_first, x_all, dz_all, h_all, da_all, db_all, g1_in, g3_in, g2_in, g1, g3, g2, s1, s3, s2, out_sem):
    del g1_in, g3_in, g2_in
    n_local = x_all.shape[0]
    n_buf = s1.shape[0]
    stage = (s1, s3, s2)
    grads = (g1, g3, g2)
    for e in range(n_first, n_local):
        slot = (e - n_first) % n_buf
        if e - n_first >= n_buf:
            for c in grad_copies(stage, grads, out_sem, e - n_buf, slot):
                c.wait()
        weight_grads((x_all, dz_all, h_all, da_all, db_all), stage, e, slot)
        for c in grad_copies(stage, grads, out_sem, e, slot):
            c.start()
    for e in range(max(n_first, n_local - n_buf), n_local):
        for c in grad_copies(stage, grads, out_sem, e, (e - n_first) % n_buf):
            c.wait()


def pair_kernel(part, mine_ref, theirs_ref, got, send_sem, recv_sem):
    ep, mate, far, far_mate = peers()
    entry_barrier((mate,))
    sends = []
    for k, owner in enumerate((far_mate, mate)):
        c = pltpu.make_async_remote_copy(src_ref=part.at[owner], dst_ref=got.at[k], send_sem=send_sem.at[k], recv_sem=recv_sem.at[k], device_id={'ep': mate}, device_id_type=MESH)
        c.start()
        sends.append(c)
    sends[0].wait_recv()
    theirs_ref[...] = part[far] + got[0]
    sends[1].wait_recv()
    mine_ref[...] = part[ep] + got[1]
    for c in sends:
        c.wait_send()


def solution(mesh):
    n_src = mesh.shape['ep']
    vmem = pl.BlockSpec(memory_space=pltpu.VMEM)
    hbm = pl.BlockSpec(memory_space=pltpu.HBM)

    def local_step(x_loc, dy_loc, ids_loc, gate_loc, slot_loc, w_gate, w_down, w_up):
        tok, top_k = ids_loc.shape
        n_local, d_model, ff = w_gate.shape
        n_exp = n_local * n_src
        cap = slot_capacity(tok, top_k, n_exp)
        rows = n_src * cap
        n_tok = n_src * tok
        dma = pltpu.SemaphoreType.DMA
        fixed = lambda v: pltpu.with_memory_space_constraint(v, pltpu.HBM)
        turned = tuple(pltpu.VMEM((n_local, w.shape[2], w.shape[1]), BF16) for w in (w_gate, w_up, w_down))
        dyg, metag, p_all, x_all, a_all, b_all, w1t, w3t, w2t = pl.pallas_call(
            functools.partial(gather_kernel, cap),
            out_shape=(
                pltpu.VMEM((n_tok, d_model), BF16),
                pltpu.VMEM((n_src, 16, 128), F32),
                pltpu.VMEM((n_local, rows, n_tok), BF16),
                pltpu.VMEM((n_local, rows, d_model), BF16),
                pltpu.VMEM((n_local, rows, ff), BF16),
                pltpu.VMEM((n_local, rows, ff), BF16),
            ) + turned,
            in_specs=[hbm] * 8,
            out_specs=(vmem,) * 9,
            scratch_shapes=[
                pltpu.VMEM((n_tok, d_model), BF16),
                pltpu.VMEM((top_k, tok), jnp.int32),
                pltpu.VMEM((top_k, tok), jnp.int32),
                pltpu.VMEM((top_k, tok), F32),
                *(pltpu.VMEM(w.shape, BF16) for w in (w_gate, w_up, w_down)),
                dma((3, n_local)),
                dma((5,)),
                dma((15,)),
                dma((15,)),
            ],
            compiler_params=pltpu.CompilerParams(collective_id=0, has_side_effects=True, vmem_limit_bytes=27 << 20),
            name='gather',
        )(*map(fixed, (x_loc, dy_loc, ids_loc.T, slot_loc.T, gate_loc.T, w_gate, w_up, w_down)))
        grad_shapes = tuple(pltpu.HBM(w.shape, F32) for w in (w_gate, w_up, w_down))
        stage = lambda n: [pltpu.VMEM((n,) + w.shape[1:], F32) for w in (w_gate, w_up, w_down)]
        row_bytes = n_local * rows * (2 * d_model + 3 * ff) * 2
        g1, g3, g2, part, dz_all, h_all, da_all, db_all = pl.pallas_call(
            functools.partial(expert_kernel, cap, N_FIRST),
            out_shape=grad_shapes + (
                pltpu.VMEM((n_src, tok, d_model), F32),
                pltpu.VMEM((n_local, rows, d_model), BF16),
                pltpu.VMEM((n_local, rows, ff), BF16),
                pltpu.VMEM((n_local, rows, ff), BF16),
                pltpu.VMEM((n_local, rows, ff), BF16),
            ),
            in_specs=[vmem] * 9,
            out_specs=(hbm,) * 3 + (vmem,) * 5,
            scratch_shapes=[pltpu.VMEM((n_local, rows, d_model), BF16), *stage(2), dma((3, 2))],
            compiler_params=pltpu.CompilerParams(vmem_limit_bytes=20 << 20),
            name='experts',
        )(dyg, metag, p_all, x_all, a_all, b_all, w1t, w3t, w2t)
        rows_in = (x_all, dz_all, h_all, da_all, db_all)
        mine, theirs = pl.pallas_call(
            pair_kernel,
            out_shape=(pltpu.VMEM((tok, d_model), F32),) * 2,
            in_specs=[vmem],
            out_specs=(vmem,) * 2,
            scratch_shapes=[pltpu.VMEM((2, tok, d_model), F32), dma((2,)), dma((2,))],
            compiler_params=pltpu.CompilerParams(collective_id=1, has_side_effects=True, vmem_limit_bytes=4 << 20),
            name='pair',
        )(part)
        far = lax.ppermute(theirs, 'ep', [(i, (i + 2) % n_src) for i in range(n_src)])
        n_rest = n_local - N_FIRST
        g1, g3, g2 = pl.pallas_call(
            functools.partial(rest_kernel, N_FIRST),
            out_shape=grad_shapes,
            in_specs=[vmem] * 5 + [hbm] * 3,
            out_specs=(hbm,) * 3,
            scratch_shapes=[*stage(N_BUF), dma((3, N_BUF))],
            input_output_aliases={5: 0, 6: 1, 7: 2},
            compiler_params=pltpu.CompilerParams(vmem_limit_bytes=40 << 20),
            cost_estimate=pl.CostEstimate(flops=2 * 3 * n_rest * rows * d_model * ff, bytes_accessed=n_rest * 3 * d_model * ff * 4 + row_bytes, transcendentals=0),
            name='rest',
        )(*rows_in, g1, g3, g2)
        dx_loc = (mine + far).astype(BF16)
        return dx_loc, g1, g2, g3

    tok_spec = P(('dp', 'ep'), None)
    w_spec = P('ep', None, None)
    grad_spec = P(('dp', 'ep'), None, None)
    return jax.shard_map(local_step, mesh=mesh, in_specs=(tok_spec, tok_spec, tok_spec, tok_spec, tok_spec, w_spec, w_spec, w_spec), out_specs=(tok_spec, grad_spec, grad_spec, grad_spec), check_vma=False)
```

time: 112 us -> 40.9 us (0.37)
  matrix products: 49.8 us -> 0 us
  Pallas kernels: 0 us -> 38.2 us
  waiting for transfers between devices: 21.2 us -> 0.01 us
  local copies, waits for them, and re-layouts: 20.5 us -> 0 us
  starting transfers between devices: 13.1 us -> 1.28 us
  other arithmetic: 6.35 us -> 0.68 us
    dot_general x8 -> x0, matrix products: 49.8 us -> none  [the longest x1 9.84 us: expert_backward(): jnp.einsum('erd,erf->edf', x_rows, d_gate, preferred_element_type=jnp.flo...]
    pallas_call x0 -> x4, Pallas kernels: none -> 38.2 us  [the longest x1 16 us: local_step(): pl.pallas_call(functools.partial(gather_kernel, cap), out_shape=(pltpu.VM...]
    all_to_all x3 -> x0, waiting for transfers between devices: 21.2 us -> none  [the longest x1 12.3 us: local_step(): lax.all_to_all(dz_send.reshape(n_exp, 1, cap_rows, d_model), 'ep', 0, 1,...]
    gather x4 -> x0, local copies, waits for them, and re-layouts: 13.4 us -> none  [the longest x1 5.01 us: source_dispatch(): jnp.take(gate_src.reshape(n_copy), slot_copy, mode='fill', fill_value=0)]
    all_to_all x3 -> x0, starting transfers between devices: 13.1 us -> none  [the longest x1 4.74 us: local_step(): lax.all_to_all(x_send.reshape(n_exp, 1, cap_rows, d_model), 'ep', 0, 1, t...]
    scatter x1 -> x0, local copies, waits for them, and re-layouts: 2.45 us -> none  [source_dispatch(): jnp.full((n_exp * cap_rows,), n_copy, jnp.int32)]
    convert_element_type x1, other arithmetic: 3 us -> 0.68 us  [local_step(): dx_loc = (mine + far).astype(BF16)]
    all_to_all x2 -> x0, local copies, waits for them, and re-layouts: 1.86 us -> none  [the longest x1 1.7 us: local_step(): lax.all_to_all(dz_send.reshape(n_exp, 1, cap_rows, d_model), 'ep', 0, 1,...]
  transfers between devices with their start and end apart: 3 -> 1, of which waited for: 3 -> 0; matrix products, arithmetic and copies ran while one was open for 33% -> 0% of each run, Pallas kernels for 0% -> 18%
where the time goes in v2:
time: 40.9 us
  Pallas kernels  38.2 us (93%)
  starting transfers between devices  1.28 us (3%)
  other arithmetic  0.68 us (2%)
  between operations  0.67 us (2%)
    pallas_call x1, Pallas kernels, local_step(): pl.pallas_call(functools.partial(gather_kernel, cap), out_shape=(pltpu.VM...  16 us
    pallas_call x1, Pallas kernels, local_step(): pl.pallas_call(functools.partial(expert_kernel, cap, N_FIRST), out_shape=...  12.9 us
    pallas_call x1, Pallas kernels, local_step(): pl.pallas_call(functools.partial(rest_kernel, N_FIRST), out_shape=grad_sh...  7.31 us
    pallas_call x1, Pallas kernels, local_step(): pl.pallas_call(pair_kernel, out_shape=(pltpu.VMEM((tok, d_model), F32),)...  2 us
    ppermute x1, starting transfers between devices, local_step(): lax.ppermute(theirs, 'ep', [(i, (i + 2) % n_src) for i in range(n_src)])  1.28 us
  transfers between devices with their start and end apart: 1, of which 0 were waited for; matrix products, arithmetic and copies ran while one was open for 0% of the time, Pallas kernels for 18%

profile of v2, /device:TPU:0, one launch (start us, length us, event | category | flops | bytes accessed | tf_op | source)
XLA Modules:
  0.0 40.9 jit_solution(1644796316138403065)
XLA Ops:
  0.6 16.0 %gather.1 = (bf16[256,1024]{1,0:T(8,128)(2,1)S(1)}, f32[4,16,128]{2,1,0:T(8,128)S(1)}, bf16[8,96,256]{2,1,0:T(8,128)(2,1)S(1)}, bf16[8,96,1024]{2,1,0:T(8,128)(2...) custom-call(bf16[64,1024]{1,0:T(8,128)(2,1)} %x_hbm.1, ...), custom_call_target="tpu_custom_call" | custom-call | tf_op jit(solution)/shard_map/gather/pallas_call | solution.py:285
  16.6 12.9 %experts.1 = (f32[8,1024,512]{2,1,0:T(8,128)}, f32[8,1024,512]{2,1,0:T(8,128)}, f32[8,512,1024]{2,1,0:T(8,128)}, f32[4,64,1024]{2,1,0:T(8,128)S(1)}, bf16[8,96,1...) custom-call(bf16[256,1024]{1,0:T(8,128)(2,1)S(1)} %get-tuple-element, ...), custom_call_target="tpu_custom_call" | custom-call | tf_op jit(solution)/shard_map/experts/pallas_call | solution.py:314
  29.6 2.0 %pair.1 = (f32[64,1024]{1,0:T(8,128)S(1)}, f32[64,1024]{1,0:T(8,128)S(1)}) custom-call(f32[4,64,1024]{2,1,0:T(8,128)S(1)} %get-tuple-element.35.part), custom_call_target="tpu_custom_call" | custom-call | tf_op jit(solution)/shard_map/pair/pallas_call | solution.py:330
  31.6 1.3 %collective-permute-start = (f32[64,1024]{1,0:T(8,128)S(1)}, f32[64,1024]{1,0:T(8,128)S(1)}, u32[]{:S(2)}, u32[]{:S(2)}) collective-permute-start(f32[64,1024]{1,0:T(8,128)S(1)} %get-tuple-element.37), channel_id=1, source_target_pairs={{0,2},{1,3},{2,0},{3,1},{4,6},{5,7},{6,4},{7,5}} | collective-permute-start | bytes 786440 | tf_op jit(solution)/shard_map/ppermute | solution.py:339
  32.8 7.3 %rest.1 = (f32[8,1024,512]{2,1,0:T(8,128)}, f32[8,1024,512]{2,1,0:T(8,128)}, f32[8,512,1024]{2,1,0:T(8,128)}) custom-call(bf16[8,96,1024]{2,1,0:T(8,128)(2,1)S(1)} %get-tuple-element.29.x_all, bf16[8,96,1024]{2,1,0:T(8,128)(2,1)S(1)} %get-tuple-element.38.dz_all, ...), custom_call_target="tpu_custom_call", output_to_operand_aliasing={{0}: (5, {}), {1}: (6, {}), {2}: (7, {})} | custom-call | flops 905969664 | bytes 24379392 | tf_op jit(solution)/shard_map/rest/pallas_call | solution.py:341
  40.2 0.0 collective-permute-done
  40.2 0.7 %add_convert_fusion = bf16[64,1024]{1,0:T(8,128)(2,1)} fusion(f32[64,1024]{1,0:T(8,128)S(1)} %get-tuple-element.36, f32[64,1024]{1,0:T(8,128)S(1)} %collective-permute-done), kind=kLoop, calls=%fused_computation | loop fusion | flops 131072 | bytes 655360 | tf_op jit(solution)/shard_map/convert_element_type | solution.py:352
Async XLA Ops:
  31.6 8.6 %collective-permute-start = (f32[64,1024]{1,0:T(8,128)S(1)}, f32[64,1024]{1,0:T(8,128)S(1)}, u32[]{:S(2)}, u32[]{:S(2)}) collective-permute-start(f32[64,1024]{1,0:T(8,128)S(1)} %get-tuple-element.37), channel_id=1, source_target_pairs={{0,2},{1,3},{2,0},{3,1},{4,6},{5,7},{6,4},{7,5}} | collective-permute-start | bytes 786440 | tf_op jit(solution)/shard_map/ppermute | solution.py:339

commit v3 on v2

--- a/solution.py
+++ b/solution.py
@@ -14,9 +14,11 @@
 NT = (((1,), (1,)), ((), ()))
 TN = (((0,), (0,)), ((), ()))
 N_FIRST = 5
-N_BUF = 4
-N_EARLY = 5
-N_MID = 4
+N_BUF = 3
+N_RING = 6
+U_ROUTE = 2
+U_PAIR = 4
+STEPS = (0, 1, 3, 4, 6)
 
 
 def slot_capacity(tok_dev, top_k, n_exp):
@@ -56,7 +58,7 @@
         lax.fori_loop(lo, hi, step, 0, unroll=unroll)
 
 
-def gather_kernel(cap, x_hbm, dy_hbm, ids_hbm, slot_hbm, gate_hbm, w1_hbm, w3_hbm, w2_hbm, dyg, metag, p_all, x_all, a_all, b_all, w1t, w3t, w2t, xg, ids_ref, slot_ref, gate_ref, w1, w3, w2, w_sem, loc_sem, send_sem, recv_sem):
+def gather_kernel(cap, x_hbm, dy_hbm, ids_hbm, slot_hbm, gate_hbm, w1_hbm, w3_hbm, w2_hbm, p_all, x_all, dz_all, a_all, b_all, w1t, w3t, w2t, xg, dyg, metag, g_rows, ids_ref, slot_ref, gate_ref, w1, w3, w2, w_sem, loc_sem, send_sem, recv_sem):
     ep, mate, far, far_mate = peers()
     n_local, rows, n_tok = p_all.shape
     n_src = metag.shape[0]
@@ -72,12 +74,19 @@
         c.start()
         small.append(c)
 
+    n_ring = w2.shape[0]
+
+    def load_w2(e):
+        return pltpu.make_async_copy(w2_hbm.at[e], w2.at[lax.rem(e, n_ring)], w_sem.at[2, e])
+
     def loads(e):
-        return [pltpu.make_async_copy(src.at[e], dst.at[e], w_sem.at[k, e]) for k, (src, dst) in enumerate(((w1_hbm, w1), (w3_hbm, w3), (w2_hbm, w2)))]
+        return [pltpu.make_async_copy(src.at[e], dst.at[e], w_sem.at[k, e]) for k, (src, dst) in enumerate(((w1_hbm, w1), (w3_hbm, w3)))]
 
     for e in range(n_local):
         for c in loads(e):
             c.start(priority=1)
+        if e < n_ring:
+            load_w2(e).start(priority=1)
     for c in small:
         c.wait()
     key = jnp.where(slot_ref[...] >= 0, ids_ref[...] * cap + slot_ref[...], -1)
@@ -98,9 +107,9 @@
     def block(ref, base, off):
         return ref.at[pl.ds(base + off, half)]
 
+    metas = [send(metag.at[ep], metag.at[ep], 12 + k, to) for k, to in enumerate((far, mate, far_mate))]
     to_far = [send(block(ref, mine, off), block(ref, mine, off), k, far) for k, (ref, off) in enumerate(pieces)]
     to_mate = [send(block(ref, mine, off), block(ref, mine, off), 4 + k, mate) for k, (ref, off) in enumerate(pieces)]
-    metas = [send(metag.at[ep], metag.at[ep], 12 + k, to) for k, to in enumerate((far, mate, far_mate))]
     r256 = lax.broadcasted_iota(jnp.int32, (256, 256), 0)
     c256 = lax.broadcasted_iota(jnp.int32, (256, 256), 1)
     eye = jnp.where(r256 == c256, 1.0, 0.0).astype(BF16)
@@ -108,10 +117,12 @@
     def turn(e):
         for c in loads(e):
             c.wait()
+        load_w2(e).wait()
         w1t[e] = w1[e].T
         w3t[e] = w3[e].T
+        slot = lax.rem(e, n_ring)
         for q in range(w2.shape[2] // 256):
-            w2t[e, q * 256:(q + 1) * 256, :] = mm(eye, w2[e, :, q * 256:(q + 1) * 256], NT).astype(BF16)
+            w2t[e, q * 256:(q + 1) * 256, :] = mm(eye, w2[slot, :, q * 256:(q + 1) * 256], NT).astype(BF16)
 
     relays = []
 
@@ -120,35 +131,66 @@
         to_far[k].wait_recv()
         relays.append(send(block(ref, theirs, off), block(ref, theirs, off), 8 + k, mate))
 
-    run(0, N_EARLY, turn, 1)
-    relay(0)
-    relay(1)
-    run(N_EARLY, n_local, turn, 1)
-    for c in to_mate[:2] + relays[:2] + metas:
+    def turn_load(e):
+        turn(e)
+        load_w2(e + n_ring).start(priority=1)
+
+    run(0, n_local - n_ring, turn_load, 1)
+    run(n_local - n_ring, 4, turn, 1)
+    for c in metas:
         c.wait_recv()
     lane = lax.broadcasted_iota(jnp.int32, (1, n_tok), 1)
     src_base = (lane // tok) * cap
     row_id = lax.broadcasted_iota(jnp.int32, (rows, n_tok), 0)
-    key = all_meta(metag, tok)[0:8, :].astype(jnp.int32)
-
-    def front(e):
+    meta = all_meta(metag, tok)
+    key = meta[0:8, :].astype(jnp.int32)
+    gate = meta[8:16, :]
+
+    def route(e):
         lo = (ep * n_local + e) * cap
         hit = (key >= lo) & (key < lo + cap)
         slot = jnp.sum(jnp.where(hit, key - lo + 1, 0), axis=0, keepdims=True)
-        want = jnp.where(slot > 0, slot - 1 + src_base, -1)
-        sel = jnp.where(row_id == want, 1.0, 0.0).astype(BF16)
-        p_all[e] = sel
-        x_rows = mm(sel, xg[...], NN).astype(BF16)
-        x_all[e] = x_rows
-        a_all[e] = mm(x_rows, w1[e], NN).astype(BF16)
-        b_all[e] = mm(x_rows, w3[e], NN).astype(BF16)
-
-    run(0, N_MID, front, 2)
+        g_tok = jnp.sum(jnp.where(hit, gate, 0.0), axis=0, keepdims=True)
+        pick = row_id == jnp.where(slot > 0, slot - 1 + src_base, -1)
+        p_all[e] = jnp.where(pick, 1.0, 0.0).astype(BF16)
+        g_rows[e] = jnp.broadcast_to(jnp.sum(jnp.where(pick, g_tok, 0.0), axis=1, keepdims=True), g_rows.shape[1:])
+
+    run(0, n_local, route, U_ROUTE)
+    turn(4)
+    relay(0)
+    relay(1)
+    turn(5)
+    for c in to_mate[:2] + relays[:2]:
+        c.wait_recv()
+
+    def spread(i):
+        two = pl.ds(i * 2, 2)
+        x_all[two] = mm(p_all[two].reshape(2 * rows, n_tok), xg[...], NN).astype(BF16).reshape(2, rows, -1)
+
+    def front(e):
+        a_all[e] = mm(x_all[e], w1[e], NN).astype(BF16)
+        b_all[e] = mm(x_all[e], w3[e], NN).astype(BF16)
+
+    run(0, n_local // 2, spread, U_PAIR)
+    front(0)
+    turn(6)
+    front(1)
+    front(2)
     relay(2)
     relay(3)
-    run(N_MID, n_local, front, 2)
+    front(3)
+    turn(7)
+    for e in range(4, n_local):
+        front(e)
     for c in to_mate[2:] + relays[2:]:
         c.wait_recv()
+
+    def scale(i):
+        two = pl.ds(i * 2, 2)
+        dy_rows = mm(p_all[two].reshape(2 * rows, n_tok), dyg[...], NN).reshape(2, rows, -1)
+        dz_all[two] = (g_rows[two][:, :, 0:1] * dy_rows).astype(BF16)
+
+    run(0, n_local // 2, scale, U_PAIR)
     for c in to_far + to_mate + relays + metas:
         c.wait_send()
 
@@ -173,26 +215,15 @@
     s3[slot] = mm(x_rows, db_all[e], TN)
 
 
-def expert_kernel(cap, n_first, dyg, metag, p_all, x_all, a_all, b_all, w1t, w3t, w2t, g1, g3, g2, part, dz_all, h_all, da_all, db_all, dx_all, s1, s3, s2, out_sem):
-    ep = lax.axis_index('ep')
+def expert_kernel(n_first, p_all, x_all, dz_all, a_all, b_all, w1t, w3t, w2t, g1, g3, g2, part, h_all, da_all, db_all, dx_all, s1, s3, s2, out_sem):
     n_local, rows, n_tok = p_all.shape
-    n_src = metag.shape[0]
-    tok = n_tok // n_src
-    meta = all_meta(metag, tok)
-    key = meta[0:8, :].astype(jnp.int32)
-    gate = meta[8:16, :]
+    n_src, tok, _ = part.shape
     rows_in = (x_all, dz_all, h_all, da_all, db_all)
     stage = (s1, s3, s2)
     grads = (g1, g3, g2)
 
     def middle(e):
-        lo = (ep * n_local + e) * cap
-        g_tok = jnp.sum(jnp.where((key >= lo) & (key < lo + cap), gate, 0.0), axis=0, keepdims=True)
-        sel = p_all[e]
-        g_row = jnp.sum(sel.astype(F32) * g_tok, axis=1, keepdims=True)
-        dz_rows = (g_row * mm(sel, dyg[...], NN)).astype(BF16)
-        dz_all[e] = dz_rows
-        dh = mm(dz_rows, w2t[e], NN)
+        dh = mm(dz_all[e], w2t[e], NN)
         a = a_all[e].astype(F32)
         b = b_all[e].astype(F32)
         sg = jax.nn.sigmoid(a)
@@ -204,26 +235,21 @@
     def back(e):
         dx_all[e] = (mm(da_all[e], w1t[e], NN) + mm(db_all[e], w3t[e], NN)).astype(BF16)
 
-    def first(e):
-        middle(e)
+    def grads_of(e):
+        if e >= 2:
+            for c in grad_copies(stage, grads, out_sem, e - 2, e % 2):
+                c.wait()
+        weight_grads(rows_in, stage, e, e % 2)
+        for c in grad_copies(stage, grads, out_sem, e, e % 2):
+            c.start()
+
+    middle(0)
+    for e in range(n_local):
+        if e + 1 < n_local:
+            middle(e + 1)
+        if e in STEPS:
+            grads_of(STEPS.index(e))
         back(e)
-        slot = lax.rem(e, 2)
-
-        @pl.when(e >= 2)
-        def _():
-            for c in grad_copies(stage, grads, out_sem, e - 2, slot):
-                c.wait()
-
-        weight_grads(rows_in, stage, e, slot)
-        for c in grad_copies(stage, grads, out_sem, e, slot):
-            c.start()
-
-    def later(e):
-        middle(e)
-        back(e)
-
-    run(0, n_first, first, 1)
-    run(n_first, n_local, later, 1)
     total = mm(p_all[...].reshape(n_local * rows, n_tok), dx_all[...].reshape(n_local * rows, -1), TN)
     for s in range(n_src):
         part[s] = total[s * tok:(s + 1) * tok]
@@ -282,50 +308,53 @@
         dma = pltpu.SemaphoreType.DMA
         fixed = lambda v: pltpu.with_memory_space_constraint(v, pltpu.HBM)
         turned = tuple(pltpu.VMEM((n_local, w.shape[2], w.shape[1]), BF16) for w in (w_gate, w_up, w_down))
-        dyg, metag, p_all, x_all, a_all, b_all, w1t, w3t, w2t = pl.pallas_call(
+        p_all, x_all, dz_all, a_all, b_all, w1t, w3t, w2t = pl.pallas_call(
             functools.partial(gather_kernel, cap),
             out_shape=(
+                pltpu.VMEM((n_local, rows, n_tok), BF16),
+                pltpu.VMEM((n_local, rows, d_model), BF16),
+                pltpu.VMEM((n_local, rows, d_model), BF16),
+                pltpu.VMEM((n_local, rows, ff), BF16),
+                pltpu.VMEM((n_local, rows, ff), BF16),
+            ) + turned,
+            in_specs=[hbm] * 8,
+            out_specs=(vmem,) * 8,
+            scratch_shapes=[
+                pltpu.VMEM((n_tok, d_model), BF16),
                 pltpu.VMEM((n_tok, d_model), BF16),
                 pltpu.VMEM((n_src, 16, 128), F32),
-                pltpu.VMEM((n_local, rows, n_tok), BF16),
-                pltpu.VMEM((n_local, rows, d_model), BF16),
-                pltpu.VMEM((n_local, rows, ff), BF16),
-                pltpu.VMEM((n_local, rows, ff), BF16),
-            ) + turned,
-            in_specs=[hbm] * 8,
-            out_specs=(vmem,) * 9,
-            scratch_shapes=[
-                pltpu.VMEM((n_tok, d_model), BF16),
+                pltpu.VMEM((n_local, rows, 128), F32),
                 pltpu.VMEM((top_k, tok), jnp.int32),
                 pltpu.VMEM((top_k, tok), jnp.int32),
                 pltpu.VMEM((top_k, tok), F32),
-                *(pltpu.VMEM(w.shape, BF16) for w in (w_gate, w_up, w_down)),
+                pltpu.VMEM(w_gate.shape, BF16),
+                pltpu.VMEM(w_up.shape, BF16),
+                pltpu.VMEM((N_RING,) + w_down.shape[1:], BF16),
                 dma((3, n_local)),
                 dma((5,)),
                 dma((15,)),
                 dma((15,)),
             ],
-            compiler_params=pltpu.CompilerParams(collective_id=0, has_side_effects=True, vmem_limit_bytes=27 << 20),
+            compiler_params=pltpu.CompilerParams(collective_id=0, has_side_effects=True, vmem_limit_bytes=24 << 20),
             name='gather',
         )(*map(fixed, (x_loc, dy_loc, ids_loc.T, slot_loc.T, gate_loc.T, w_gate, w_up, w_down)))
         grad_shapes = tuple(pltpu.HBM(w.shape, F32) for w in (w_gate, w_up, w_down))
         stage = lambda n: [pltpu.VMEM((n,) + w.shape[1:], F32) for w in (w_gate, w_up, w_down)]
         row_bytes = n_local * rows * (2 * d_model + 3 * ff) * 2
-        g1, g3, g2, part, dz_all, h_all, da_all, db_all = pl.pallas_call(
-            functools.partial(expert_kernel, cap, N_FIRST),
+        g1, g3, g2, part, h_all, da_all, db_all = pl.pallas_call(
+            functools.partial(expert_kernel, N_FIRST),
             out_shape=grad_shapes + (
                 pltpu.VMEM((n_src, tok, d_model), F32),
-                pltpu.VMEM((n_local, rows, d_model), BF16),
                 pltpu.VMEM((n_local, rows, ff), BF16),
                 pltpu.VMEM((n_local, rows, ff), BF16),
                 pltpu.VMEM((n_local, rows, ff), BF16),
             ),
-            in_specs=[vmem] * 9,
-            out_specs=(hbm,) * 3 + (vmem,) * 5,
+            in_specs=[vmem] * 8,
+            out_specs=(hbm,) * 3 + (vmem,) * 4,
             scratch_shapes=[pltpu.VMEM((n_local, rows, d_model), BF16), *stage(2), dma((3, 2))],
             compiler_params=pltpu.CompilerParams(vmem_limit_bytes=20 << 20),
             name='experts',
-        )(dyg, metag, p_all, x_all, a_all, b_all, w1t, w3t, w2t)
+        )(p_all, x_all, dz_all, a_all, b_all, w1t, w3t, w2t)
         rows_in = (x_all, dz_all, h_all, da_all, db_all)
         mine, theirs = pl.pallas_call(
             pair_kernel,
@@ -345,7 +374,7 @@
             out_specs=(hbm,) * 3,
             scratch_shapes=[*stage(N_BUF), dma((3, N_BUF))],
             input_output_aliases={5: 0, 6: 1, 7: 2},
-            compiler_params=pltpu.CompilerParams(vmem_limit_bytes=40 << 20),
+            compiler_params=pltpu.CompilerParams(vmem_limit_bytes=20 << 20),
             cost_estimate=pl.CostEstimate(flops=2 * 3 * n_rest * rows * d_model * ff, bytes_accessed=n_rest * 3 * d_model * ff * 4 + row_bytes, transcendentals=0),
             name='rest',
         )(*rows_in, g1, g3, g2)

time: 40.9 us -> 39 us (0.954)
  Pallas kernels: 38.2 us -> 36.3 us
  waiting for transfers between devices: 0.01 us -> 0.42 us
    pallas_call x1, Pallas kernels: 12.9 us -> 11.4 us  [local_step(): pl.pallas_call(functools.partial(expert_kernel, N_FIRST), out_shape=grad_...]
    pallas_call x1, Pallas kernels: 16 us -> 15.4 us  [local_step(): pl.pallas_call(functools.partial(gather_kernel, cap), out_shape=(pltpu.VM...]
    ppermute x1, waiting for transfers between devices: 0.01 us -> 0.42 us  [local_step(): lax.ppermute(theirs, 'ep', [(i, (i + 2) % n_src) for i in range(n_src)])]
  transfers between devices with their start and end apart: 1 -> 1, of which waited for: 0 -> 1; matrix products, arithmetic and copies ran while one was open for 0% -> 0% of each run, Pallas kernels for 18% -> 19%
where the time goes in v3:
time: 39 us; the launch traced here: 38.9 us
  Pallas kernels  36.3 us (93%)
  starting transfers between devices  0.92 us (2%)
  other arithmetic  0.68 us (2%)
  between operations  0.67 us (2%)
  waiting for transfers between devices  0.42 us (1%)
    pallas_call x1, Pallas kernels, local_step(): pl.pallas_call(functools.partial(gather_kernel, cap), out_shape=(pltpu.VM...  15.4 us
    pallas_call x1, Pallas kernels, local_step(): pl.pallas_call(functools.partial(expert_kernel, N_FIRST), out_shape=grad_...  11.4 us
    pallas_call x1, Pallas kernels, local_step(): pl.pallas_call(functools.partial(rest_kernel, N_FIRST), out_shape=grad_sh...  7.29 us
    pallas_call x1, Pallas kernels, local_step(): pl.pallas_call(pair_kernel, out_shape=(pltpu.VMEM((tok, d_model), F32),)...  2.16 us
    ppermute x1, starting transfers between devices, local_step(): lax.ppermute(theirs, 'ep', [(i, (i + 2) % n_src) for i in range(n_src)])  0.92 us
  transfers between devices with their start and end apart: 1, of which 1 were waited for; matrix products, arithmetic and copies ran while one was open for 0% of the time, Pallas kernels for 19%

profile of v3, /device:TPU:0, one launch (start us, length us, event | category | flops | bytes accessed | tf_op | source)
XLA Modules:
  0.0 38.9 jit_solution(81756106902362296)
XLA Ops:
  0.6 15.4 %gather.1 = (bf16[8,96,256]{2,1,0:T(8,128)(2,1)S(1)}, bf16[8,96,1024]{2,1,0:T(8,128)(2,1)S(1)}, bf16[8,96,1024]{2,1,0:T(8,128)(2,1)S(1)}, bf16[8,96,512]{2,1,0:T...) custom-call(bf16[64,1024]{1,0:T(8,128)(2,1)} %x_hbm.1, ...), custom_call_target="tpu_custom_call" | custom-call | tf_op jit(solution)/shard_map/gather/pallas_call | solution.py:311
  16.1 11.4 %experts.1 = (f32[8,1024,512]{2,1,0:T(8,128)}, f32[8,1024,512]{2,1,0:T(8,128)}, f32[8,512,1024]{2,1,0:T(8,128)}, f32[4,64,1024]{2,1,0:T(8,128)S(1)}, bf16[8,96,5...) custom-call(bf16[8,96,256]{2,1,0:T(8,128)(2,1)S(1)} %get-tuple-element.24.p_all, ...), custom_call_target="tpu_custom_call" | custom-call | tf_op jit(solution)/shard_map/experts/pallas_call | solution.py:344
  27.5 2.2 %pair.1 = (f32[64,1024]{1,0:T(8,128)S(1)}, f32[64,1024]{1,0:T(8,128)S(1)}) custom-call(f32[4,64,1024]{2,1,0:T(8,128)S(1)} %get-tuple-element.32.part), custom_call_target="tpu_custom_call" | custom-call | tf_op jit(solution)/shard_map/pair/pallas_call | solution.py:359
  29.6 0.9 %collective-permute-start = (f32[64,1024]{1,0:T(8,128)S(1)}, f32[64,1024]{1,0:T(8,128)S(1)}, u32[]{:S(2)}, u32[]{:S(2)}) collective-permute-start(f32[64,1024]{1,0:T(8,128)S(1)} %get-tuple-element.34), channel_id=1, source_target_pairs={{0,2},{1,3},{2,0},{3,1},{4,6},{5,7},{6,4},{7,5}} | collective-permute-start | bytes 786440 | tf_op jit(solution)/shard_map/ppermute | solution.py:368
  30.5 7.3 %rest.1 = (f32[8,1024,512]{2,1,0:T(8,128)}, f32[8,1024,512]{2,1,0:T(8,128)}, f32[8,512,1024]{2,1,0:T(8,128)}) custom-call(bf16[8,96,1024]{2,1,0:T(8,128)(2,1)S(1)} %get-tuple-element.25.x_all, bf16[8,96,1024]{2,1,0:T(8,128)(2,1)S(1)} %get-tuple-element.26.dz_all, ...), custom_call_target="tpu_custom_call", output_to_operand_aliasing={{0}: (5, {}), {1}: (6, {}), {2}: (7, {})} | custom-call | flops 905969664 | bytes 24379392 | tf_op jit(solution)/shard_map/rest/pallas_call | solution.py:370
  37.8 0.4 %collective-permute-done = f32[64,1024]{1,0:T(8,128)S(1)} collective-permute-done((f32[64,1024]{1,0:T(8,128)S(1)}, f32[64,1024]{1,0:T(8,128)S(1)}, u32[]{:S(2)}, u32[]{:S(2)}) %collective-permute-start) | collective-permute-done | bytes 262176 | tf_op jit(solution)/shard_map/ppermute | solution.py:368
  38.3 0.7 %add_convert_fusion = bf16[64,1024]{1,0:T(8,128)(2,1)} fusion(f32[64,1024]{1,0:T(8,128)S(1)} %get-tuple-element.33, f32[64,1024]{1,0:T(8,128)S(1)} %collective-permute-done), kind=kLoop, calls=%fused_computation | loop fusion | flops 131072 | bytes 655360 | tf_op jit(solution)/shard_map/convert_element_type | solution.py:381
Async XLA Ops:
  29.6 8.6 %collective-permute-start = (f32[64,1024]{1,0:T(8,128)S(1)}, f32[64,1024]{1,0:T(8,128)S(1)}, u32[]{:S(2)}, u32[]{:S(2)}) collective-permute-start(f32[64,1024]{1,0:T(8,128)S(1)} %get-tuple-element.34), channel_id=1, source_target_pairs={{0,2},{1,3},{2,0},{3,1},{4,6},{5,7},{6,4},{7,5}} | collective-permute-start | bytes 786440 | tf_op jit(solution)/shard_map/ppermute | solution.py:368

commit v4 on v3

--- a/solution.py
+++ b/solution.py
@@ -15,10 +15,11 @@
 TN = (((0,), (0,)), ((), ()))
 N_FIRST = 5
 N_BUF = 3
+N_STAGE = 2
 N_RING = 6
 U_ROUTE = 2
 U_PAIR = 4
-STEPS = (0, 1, 3, 4, 6)
+STEPS = (0, 1, 2, 4, 5)
 
 
 def slot_capacity(tok_dev, top_k, n_exp):
@@ -114,15 +115,20 @@
     c256 = lax.broadcasted_iota(jnp.int32, (256, 256), 1)
     eye = jnp.where(r256 == c256, 1.0, 0.0).astype(BF16)
 
-    def turn(e):
+    def ready(e):
         for c in loads(e):
             c.wait()
         load_w2(e).wait()
+
+    def flip(e):
         w1t[e] = w1[e].T
         w3t[e] = w3[e].T
         slot = lax.rem(e, n_ring)
-        for q in range(w2.shape[2] // 256):
-            w2t[e, q * 256:(q + 1) * 256, :] = mm(eye, w2[slot, :, q * 256:(q + 1) * 256], NT).astype(BF16)
+        w2t[e] = w2[slot].T
+
+    def turn(e):
+        ready(e)
+        flip(e)
 
     relays = []
 
@@ -171,16 +177,18 @@
         a_all[e] = mm(x_all[e], w1[e], NN).astype(BF16)
         b_all[e] = mm(x_all[e], w3[e], NN).astype(BF16)
 
-    run(0, n_local // 2, spread, U_PAIR)
+    ready(6)
+    for i in range(n_local // 2):
+        spread(i)
     front(0)
-    turn(6)
+    flip(6)
     front(1)
-    front(2)
     relay(2)
     relay(3)
-    front(3)
-    turn(7)
-    for e in range(4, n_local):
+    ready(7)
+    front(2)
+    flip(7)
+    for e in range(3, n_local):
         front(e)
     for c in to_mate[2:] + relays[2:]:
         c.wait_recv()
@@ -202,17 +210,17 @@
     return jnp.concatenate(halves, axis=1)
 
 
-def grad_copies(stage, grads, out_sem, e, slot):
-    return [pltpu.make_async_copy(s.at[slot], g.at[e], out_sem.at[k, slot]) for k, (s, g) in enumerate(zip(stage, grads))]
-
-
-def weight_grads(rows_in, stage, e, slot):
+def grad_copy(stage, grads, out_sem, k, e, slot):
+    return pltpu.make_async_copy(stage[k].at[slot], grads[k].at[e], out_sem.at[k, slot])
+
+
+def weight_grad(rows_in, stage, grads, out_sem, k, e, slot, prev):
     x_all, dz_all, h_all, da_all, db_all = rows_in
-    s1, s3, s2 = stage
-    x_rows = x_all[e]
-    s2[slot] = mm(h_all[e], dz_all[e], TN)
-    s1[slot] = mm(x_rows, da_all[e], TN)
-    s3[slot] = mm(x_rows, db_all[e], TN)
+    if prev >= 0:
+        grad_copy(stage, grads, out_sem, k, prev, slot).wait()
+    left, right = ((x_all, da_all), (x_all, db_all), (h_all, dz_all))[k]
+    stage[k][slot] = mm(left[e], right[e], TN)
+    grad_copy(stage, grads, out_sem, k, e, slot).start()
 
 
 def expert_kernel(n_first, p_all, x_all, dz_all, a_all, b_all, w1t, w3t, w2t, g1, g3, g2, part, h_all, da_all, db_all, dx_all, s1, s3, s2, out_sem):
@@ -222,40 +230,42 @@
     stage = (s1, s3, s2)
     grads = (g1, g3, g2)
 
-    def middle(e):
-        dh = mm(dz_all[e], w2t[e], NN)
+    def grad(k, e):
+        weight_grad(rows_in, stage, grads, out_sem, k, e, e % N_STAGE, e - N_STAGE)
+
+    def hidden(e):
         a = a_all[e].astype(F32)
         b = b_all[e].astype(F32)
         sg = jax.nn.sigmoid(a)
         silu = a * sg
         h_all[e] = (silu * b).astype(BF16)
-        da_all[e] = (dh * b * sg * (1.0 + a * (1.0 - sg))).astype(BF16)
+        return b, sg, silu, 1.0 + a * (1.0 - sg)
+
+    def middle(e, early=False):
+        b, sg, silu, slope = hidden(e)
+        if early:
+            grad(2, e)
+        dh = mm(dz_all[e], w2t[e], NN)
+        da_all[e] = (dh * b * sg * slope).astype(BF16)
         db_all[e] = (dh * silu).astype(BF16)
 
     def back(e):
         dx_all[e] = (mm(da_all[e], w1t[e], NN) + mm(db_all[e], w3t[e], NN)).astype(BF16)
 
-    def grads_of(e):
-        if e >= 2:
-            for c in grad_copies(stage, grads, out_sem, e - 2, e % 2):
-                c.wait()
-        weight_grads(rows_in, stage, e, e % 2)
-        for c in grad_copies(stage, grads, out_sem, e, e % 2):
-            c.start()
-
-    middle(0)
+    middle(0, True)
     for e in range(n_local):
+        if e in STEPS:
+            for k in (2, 0, 1) if e else (0, 1):
+                grad(k, STEPS.index(e))
         if e + 1 < n_local:
             middle(e + 1)
-        if e in STEPS:
-            grads_of(STEPS.index(e))
         back(e)
     total = mm(p_all[...].reshape(n_local * rows, n_tok), dx_all[...].reshape(n_local * rows, -1), TN)
     for s in range(n_src):
         part[s] = total[s * tok:(s + 1) * tok]
-    for e in range(max(n_first - 2, 0), n_first):
-        for c in grad_copies(stage, grads, out_sem, e, e % 2):
-            c.wait()
+    for e in range(max(n_first - N_STAGE, 0), n_first):
+        for k in range(3):
+            grad_copy(stage, grads, out_sem, k, e, e % N_STAGE).wait()
 
 
 def rest_kernel(n_first, x_all, dz_all, h_all, da_all, db_all, g1_in, g3_in, g2_in, g1, g3, g2, s1, s3, s2, out_sem):
@@ -264,17 +274,13 @@
     n_buf = s1.shape[0]
     stage = (s1, s3, s2)
     grads = (g1, g3, g2)
+    rows_in = (x_all, dz_all, h_all, da_all, db_all)
     for e in range(n_first, n_local):
-        slot = (e - n_first) % n_buf
-        if e - n_first >= n_buf:
-            for c in grad_copies(stage, grads, out_sem, e - n_buf, slot):
-                c.wait()
-        weight_grads((x_all, dz_all, h_all, da_all, db_all), stage, e, slot)
-        for c in grad_copies(stage, grads, out_sem, e, slot):
-            c.start()
+        for k in (2, 0, 1):
+            weight_grad(rows_in, stage, grads, out_sem, k, e, (e - n_first) % n_buf, e - n_buf if e - n_buf >= n_first else -1)
     for e in range(max(n_first, n_local - n_buf), n_local):
-        for c in grad_copies(stage, grads, out_sem, e, (e - n_first) % n_buf):
-            c.wait()
+        for k in range(3):
+            grad_copy(stage, grads, out_sem, k, e, (e - n_first) % n_buf).wait()
 
 
 def pair_kernel(part, mine_ref, theirs_ref, got, send_sem, recv_sem):
@@ -335,7 +341,7 @@
                 dma((15,)),
                 dma((15,)),
             ],
-            compiler_params=pltpu.CompilerParams(collective_id=0, has_side_effects=True, vmem_limit_bytes=24 << 20),
+            compiler_params=pltpu.CompilerParams(collective_id=0, has_side_effects=True, vmem_limit_bytes=25 << 20),
             name='gather',
         )(*map(fixed, (x_loc, dy_loc, ids_loc.T, slot_loc.T, gate_loc.T, w_gate, w_up, w_down)))
         grad_shapes = tuple(pltpu.HBM(w.shape, F32) for w in (w_gate, w_up, w_down))
@@ -351,7 +357,7 @@
             ),
             in_specs=[vmem] * 8,
             out_specs=(hbm,) * 3 + (vmem,) * 4,
-            scratch_shapes=[pltpu.VMEM((n_local, rows, d_model), BF16), *stage(2), dma((3, 2))],
+            scratch_shapes=[pltpu.VMEM((n_local, rows, d_model), BF16), *stage(N_STAGE), dma((3, N_STAGE))],
             compiler_params=pltpu.CompilerParams(vmem_limit_bytes=20 << 20),
             name='experts',
         )(p_all, x_all, dz_all, a_all, b_all, w1t, w3t, w2t)

time: 39 us -> 37.9 us (0.972)
  Pallas kernels: 36.3 us -> 34.9 us
  starting transfers between devices: 0.92 us -> 1.47 us
    pallas_call x1, Pallas kernels: 15.4 us -> 14.8 us  [local_step(): pl.pallas_call(functools.partial(gather_kernel, cap), out_shape=(pltpu.VM...]
    ppermute x1, starting transfers between devices: 0.92 us -> 1.47 us  [local_step(): lax.ppermute(theirs, 'ep', [(i, (i + 2) % n_src) for i in range(n_src)])]
where the time goes in v4:
time: 37.9 us; the launch traced here: 37.8 us
  Pallas kernels  34.9 us (92%)
  starting transfers between devices  1.47 us (4%)
  other arithmetic  0.68 us (2%)
  between operations  0.67 us (2%)
    pallas_call x1, Pallas kernels, local_step(): pl.pallas_call(functools.partial(gather_kernel, cap), out_shape=(pltpu.VM...  14.8 us
    pallas_call x1, Pallas kernels, local_step(): pl.pallas_call(functools.partial(expert_kernel, N_FIRST), out_shape=grad_...  11.1 us
    pallas_call x1, Pallas kernels, local_step(): pl.pallas_call(functools.partial(rest_kernel, N_FIRST), out_shape=grad_sh...  7.02 us
    pallas_call x1, Pallas kernels, local_step(): pl.pallas_call(pair_kernel, out_shape=(pltpu.VMEM((tok, d_model), F32),)...  2 us
    ppermute x1, starting transfers between devices, local_step(): lax.ppermute(theirs, 'ep', [(i, (i + 2) % n_src) for i in range(n_src)])  1.47 us
  transfers between devices with their start and end apart: 1, of which 1 were waited for; matrix products, arithmetic and copies ran while one was open for 0% of the time, Pallas kernels for 19%

profile of v4, /device:TPU:0, one launch (start us, length us, event | category | flops | bytes accessed | tf_op | source)
XLA Modules:
  0.0 37.8 jit_solution(5351535420994214663)
XLA Ops:
  0.6 14.8 %gather.1 = (bf16[8,96,256]{2,1,0:T(8,128)(2,1)S(1)}, bf16[8,96,1024]{2,1,0:T(8,128)(2,1)S(1)}, bf16[8,96,1024]{2,1,0:T(8,128)(2,1)S(1)}, bf16[8,96,512]{2,1,0:T...) custom-call(bf16[64,1024]{1,0:T(8,128)(2,1)} %x_hbm.1, ...), custom_call_target="tpu_custom_call" | custom-call | tf_op jit(solution)/shard_map/gather/pallas_call | solution.py:317
  15.4 11.1 %experts.1 = (f32[8,1024,512]{2,1,0:T(8,128)}, f32[8,1024,512]{2,1,0:T(8,128)}, f32[8,512,1024]{2,1,0:T(8,128)}, f32[4,64,1024]{2,1,0:T(8,128)S(1)}, bf16[8,96,5...) custom-call(bf16[8,96,256]{2,1,0:T(8,128)(2,1)S(1)} %get-tuple-element.24.p_all, ...), custom_call_target="tpu_custom_call" | custom-call | tf_op jit(solution)/shard_map/experts/pallas_call | solution.py:350
  26.6 2.0 %pair.1 = (f32[64,1024]{1,0:T(8,128)S(1)}, f32[64,1024]{1,0:T(8,128)S(1)}) custom-call(f32[4,64,1024]{2,1,0:T(8,128)S(1)} %get-tuple-element.32.part), custom_call_target="tpu_custom_call" | custom-call | tf_op jit(solution)/shard_map/pair/pallas_call | solution.py:365
  28.6 1.5 %collective-permute-start = (f32[64,1024]{1,0:T(8,128)S(1)}, f32[64,1024]{1,0:T(8,128)S(1)}, u32[]{:S(2)}, u32[]{:S(2)}) collective-permute-start(f32[64,1024]{1,0:T(8,128)S(1)} %get-tuple-element.34), channel_id=1, source_target_pairs={{0,2},{1,3},{2,0},{3,1},{4,6},{5,7},{6,4},{7,5}} | collective-permute-start | bytes 786440 | tf_op jit(solution)/shard_map/ppermute | solution.py:374
  30.0 7.0 %rest.1 = (f32[8,1024,512]{2,1,0:T(8,128)}, f32[8,1024,512]{2,1,0:T(8,128)}, f32[8,512,1024]{2,1,0:T(8,128)}) custom-call(bf16[8,96,1024]{2,1,0:T(8,128)(2,1)S(1)} %get-tuple-element.25.x_all, bf16[8,96,1024]{2,1,0:T(8,128)(2,1)S(1)} %get-tuple-element.26.dz_all, ...), custom_call_target="tpu_custom_call", output_to_operand_aliasing={{0}: (5, {}), {1}: (6, {}), {2}: (7, {})} | custom-call | flops 905969664 | bytes 24379392 | tf_op jit(solution)/shard_map/rest/pallas_call | solution.py:376
  37.1 0.1 collective-permute-done
  37.1 0.7 %add_convert_fusion = bf16[64,1024]{1,0:T(8,128)(2,1)} fusion(f32[64,1024]{1,0:T(8,128)S(1)} %get-tuple-element.33, f32[64,1024]{1,0:T(8,128)S(1)} %collective-permute-done), kind=kLoop, calls=%fused_computation | loop fusion | flops 131072 | bytes 655360 | tf_op jit(solution)/shard_map/convert_element_type | solution.py:387
Async XLA Ops:
  28.6 8.6 %collective-permute-start = (f32[64,1024]{1,0:T(8,128)S(1)}, f32[64,1024]{1,0:T(8,128)S(1)}, u32[]{:S(2)}, u32[]{:S(2)}) collective-permute-start(f32[64,1024]{1,0:T(8,128)S(1)} %get-tuple-element.34), channel_id=1, source_target_pairs={{0,2},{1,3},{2,0},{3,1},{4,6},{5,7},{6,4},{7,5}} | collective-permute-start | bytes 786440 | tf_op jit(solution)/shard_map/ppermute | solution.py:374

commit v5 on v4

--- a/solution.py
+++ b/solution.py
@@ -16,6 +16,7 @@
 N_FIRST = 5
 N_BUF = 3
 N_STAGE = 2
+TAIL_ROWS = 16
 N_RING = 6
 U_ROUTE = 2
 U_PAIR = 4
@@ -103,17 +104,18 @@
         return c
 
     half = tok // 2
-    pieces = [(ref, h * half) for ref in (xg, dyg) for h in range(2)]
-
-    def block(ref, base, off):
-        return ref.at[pl.ds(base + off, half)]
+    tail = TAIL_ROWS
+    pieces = [(xg, 0, half), (xg, half, half), (dyg, 0, tok - tail), (dyg, tok - tail, tail)]
+
+    def block(k, base):
+        ref, off, size = pieces[k]
+        return ref.at[pl.ds(base + off, size)]
 
     metas = [send(metag.at[ep], metag.at[ep], 12 + k, to) for k, to in enumerate((far, mate, far_mate))]
-    to_far = [send(block(ref, mine, off), block(ref, mine, off), k, far) for k, (ref, off) in enumerate(pieces)]
-    to_mate = [send(block(ref, mine, off), block(ref, mine, off), 4 + k, mate) for k, (ref, off) in enumerate(pieces)]
-    r256 = lax.broadcasted_iota(jnp.int32, (256, 256), 0)
-    c256 = lax.broadcasted_iota(jnp.int32, (256, 256), 1)
-    eye = jnp.where(r256 == c256, 1.0, 0.0).astype(BF16)
+    to_far = [send(block(k, mine), block(k, mine), k, far) for k in range(4)]
+    direct = send(block(3, mine), block(3, mine), 11, far_mate)
+    relays = []
+    to_mate = [send(block(k, mine), block(k, mine), 4 + k, mate) for k in range(4)]
 
     def ready(e):
         for c in loads(e):
@@ -130,12 +132,9 @@
         ready(e)
         flip(e)
 
-    relays = []
-
     def relay(k):
-        ref, off = pieces[k]
         to_far[k].wait_recv()
-        relays.append(send(block(ref, theirs, off), block(ref, theirs, off), 8 + k, mate))
+        relays.append(send(block(k, theirs), block(k, theirs), 8 + k, mate))
 
     def turn_load(e):
         turn(e)
@@ -161,11 +160,13 @@
         p_all[e] = jnp.where(pick, 1.0, 0.0).astype(BF16)
         g_rows[e] = jnp.broadcast_to(jnp.sum(jnp.where(pick, g_tok, 0.0), axis=1, keepdims=True), g_rows.shape[1:])
 
-    run(0, n_local, route, U_ROUTE)
     turn(4)
     relay(0)
     relay(1)
-    turn(5)
+    ready(5)
+    for e in range(n_local):
+        route(e)
+    flip(5)
     for c in to_mate[:2] + relays[:2]:
         c.wait_recv()
 
@@ -184,13 +185,13 @@
     flip(6)
     front(1)
     relay(2)
-    relay(3)
+    relays.append(direct)
     ready(7)
     front(2)
     flip(7)
     for e in range(3, n_local):
         front(e)
-    for c in to_mate[2:] + relays[2:]:
+    for c in to_mate[2:] + relays[2:] + to_far[3:]:
         c.wait_recv()
 
     def scale(i):

time: 37.9 us -> 37.9 us (level)
  no operation moved by 1% of the time
where the time goes in v5:
time: 37.9 us; the launch traced here: 37.8 us
  Pallas kernels  35.1 us (93%)
  starting transfers between devices  1.33 us (4%)
  other arithmetic  0.68 us (2%)
  between operations  0.67 us (2%)
    pallas_call x1, Pallas kernels, local_step(): pl.pallas_call(functools.partial(gather_kernel, cap), out_shape=(pltpu.VM...  14.9 us
    pallas_call x1, Pallas kernels, local_step(): pl.pallas_call(functools.partial(expert_kernel, N_FIRST), out_shape=grad_...  11.1 us
    pallas_call x1, Pallas kernels, local_step(): pl.pallas_call(functools.partial(rest_kernel, N_FIRST), out_shape=grad_sh...  7.02 us
    pallas_call x1, Pallas kernels, local_step(): pl.pallas_call(pair_kernel, out_shape=(pltpu.VMEM((tok, d_model), F32),)...  2 us
    ppermute x1, starting transfers between devices, local_step(): lax.ppermute(theirs, 'ep', [(i, (i + 2) % n_src) for i in range(n_src)])  1.33 us
  transfers between devices with their start and end apart: 1, of which 1 were waited for; matrix products, arithmetic and copies ran while one was open for 0% of the time, Pallas kernels for 19%

profile of v5, /device:TPU:0, one launch (start us, length us, event | category | flops | bytes accessed | tf_op | source)
XLA Modules:
  0.0 37.8 jit_solution(10227327054652878890)
XLA Ops:
  0.6 14.9 %gather.1 = (bf16[8,96,256]{2,1,0:T(8,128)(2,1)S(1)}, bf16[8,96,1024]{2,1,0:T(8,128)(2,1)S(1)}, bf16[8,96,1024]{2,1,0:T(8,128)(2,1)S(1)}, bf16[8,96,512]{2,1,0:T...) custom-call(bf16[64,1024]{1,0:T(8,128)(2,1)} %x_hbm.1, ...), custom_call_target="tpu_custom_call" | custom-call | tf_op jit(solution)/shard_map/gather/pallas_call | solution.py:318
  15.6 11.1 %experts.1 = (f32[8,1024,512]{2,1,0:T(8,128)}, f32[8,1024,512]{2,1,0:T(8,128)}, f32[8,512,1024]{2,1,0:T(8,128)}, f32[4,64,1024]{2,1,0:T(8,128)S(1)}, bf16[8,96,5...) custom-call(bf16[8,96,256]{2,1,0:T(8,128)(2,1)S(1)} %get-tuple-element.24.p_all, ...), custom_call_target="tpu_custom_call" | custom-call | tf_op jit(solution)/shard_map/experts/pallas_call | solution.py:351
  26.7 2.0 %pair.1 = (f32[64,1024]{1,0:T(8,128)S(1)}, f32[64,1024]{1,0:T(8,128)S(1)}) custom-call(f32[4,64,1024]{2,1,0:T(8,128)S(1)} %get-tuple-element.32.part), custom_call_target="tpu_custom_call" | custom-call | tf_op jit(solution)/shard_map/pair/pallas_call | solution.py:366
  28.7 1.3 %collective-permute-start = (f32[64,1024]{1,0:T(8,128)S(1)}, f32[64,1024]{1,0:T(8,128)S(1)}, u32[]{:S(2)}, u32[]{:S(2)}) collective-permute-start(f32[64,1024]{1,0:T(8,128)S(1)} %get-tuple-element.34), channel_id=1, source_target_pairs={{0,2},{1,3},{2,0},{3,1},{4,6},{5,7},{6,4},{7,5}} | collective-permute-start | bytes 786440 | tf_op jit(solution)/shard_map/ppermute | solution.py:375
  30.0 7.0 %rest.1 = (f32[8,1024,512]{2,1,0:T(8,128)}, f32[8,1024,512]{2,1,0:T(8,128)}, f32[8,512,1024]{2,1,0:T(8,128)}) custom-call(bf16[8,96,1024]{2,1,0:T(8,128)(2,1)S(1)} %get-tuple-element.25.x_all, bf16[8,96,1024]{2,1,0:T(8,128)(2,1)S(1)} %get-tuple-element.26.dz_all, ...), custom_call_target="tpu_custom_call", output_to_operand_aliasing={{0}: (5, {}), {1}: (6, {}), {2}: (7, {})} | custom-call | flops 905969664 | bytes 24379392 | tf_op jit(solution)/shard_map/rest/pallas_call | solution.py:377
  37.1 0.1 collective-permute-done
  37.1 0.7 %add_convert_fusion = bf16[64,1024]{1,0:T(8,128)(2,1)} fusion(f32[64,1024]{1,0:T(8,128)S(1)} %get-tuple-element.33, f32[64,1024]{1,0:T(8,128)S(1)} %collective-permute-done), kind=kLoop, calls=%fused_computation | loop fusion | flops 131072 | bytes 655360 | tf_op jit(solution)/shard_map/convert_element_type | solution.py:388
Async XLA Ops:
  28.7 8.4 %collective-permute-start = (f32[64,1024]{1,0:T(8,128)S(1)}, f32[64,1024]{1,0:T(8,128)S(1)}, u32[]{:S(2)}, u32[]{:S(2)}) collective-permute-start(f32[64,1024]{1,0:T(8,128)S(1)} %get-tuple-element.34), channel_id=1, source_target_pairs={{0,2},{1,3},{2,0},{3,1},{4,6},{5,7},{6,4},{7,5}} | collective-permute-start | bytes 786440 | tf_op jit(solution)/shard_map/ppermute | solution.py:375

commit v6 on v5

--- a/solution.py
+++ b/solution.py
@@ -189,7 +189,7 @@
     ready(7)
     front(2)
     flip(7)
-    for e in range(3, n_local):
+    for e in range(3, 6):
         front(e)
     for c in to_mate[2:] + relays[2:] + to_far[3:]:
         c.wait_recv()
@@ -199,7 +199,10 @@
         dy_rows = mm(p_all[two].reshape(2 * rows, n_tok), dyg[...], NN).reshape(2, rows, -1)
         dz_all[two] = (g_rows[two][:, :, 0:1] * dy_rows).astype(BF16)
 
-    run(0, n_local // 2, scale, U_PAIR)
+    for i in range(n_local // 2):
+        scale(i)
+        if 6 + i < n_local:
+            front(6 + i)
     for c in to_far + to_mate + relays + metas:
         c.wait_send()
 

time: 37.9 us -> 37.9 us (level)
  no operation moved by 1% of the time
where the time goes in v6:
time: 37.9 us; the launch traced here: 37.8 us
  Pallas kernels  35.1 us (93%)
  starting transfers between devices  1.3 us (3%)
  other arithmetic  0.68 us (2%)
  between operations  0.67 us (2%)
    pallas_call x1, Pallas kernels, local_step(): pl.pallas_call(functools.partial(gather_kernel, cap), out_shape=(pltpu.VM...  14.9 us
    pallas_call x1, Pallas kernels, local_step(): pl.pallas_call(functools.partial(expert_kernel, N_FIRST), out_shape=grad_...  11.1 us
    pallas_call x1, Pallas kernels, local_step(): pl.pallas_call(functools.partial(rest_kernel, N_FIRST), out_shape=grad_sh...  7.02 us
    pallas_call x1, Pallas kernels, local_step(): pl.pallas_call(pair_kernel, out_shape=(pltpu.VMEM((tok, d_model), F32),)...  2 us
    ppermute x1, starting transfers between devices, local_step(): lax.ppermute(theirs, 'ep', [(i, (i + 2) % n_src) for i in range(n_src)])  1.3 us
  transfers between devices with their start and end apart: 1, of which 1 were waited for; matrix products, arithmetic and copies ran while one was open for 0% of the time, Pallas kernels for 19%

profile of v6, /device:TPU:0, one launch (start us, length us, event | category | flops | bytes accessed | tf_op | source)
XLA Modules:
  0.0 37.8 jit_solution(3625792484922183327)
XLA Ops:
  0.6 14.9 %gather.1 = (bf16[8,96,256]{2,1,0:T(8,128)(2,1)S(1)}, bf16[8,96,1024]{2,1,0:T(8,128)(2,1)S(1)}, bf16[8,96,1024]{2,1,0:T(8,128)(2,1)S(1)}, bf16[8,96,512]{2,1,0:T...) custom-call(bf16[64,1024]{1,0:T(8,128)(2,1)} %x_hbm.1, ...), custom_call_target="tpu_custom_call" | custom-call | tf_op jit(solution)/shard_map/gather/pallas_call | solution.py:321
  15.6 11.1 %experts.1 = (f32[8,1024,512]{2,1,0:T(8,128)}, f32[8,1024,512]{2,1,0:T(8,128)}, f32[8,512,1024]{2,1,0:T(8,128)}, f32[4,64,1024]{2,1,0:T(8,128)S(1)}, bf16[8,96,5...) custom-call(bf16[8,96,256]{2,1,0:T(8,128)(2,1)S(1)} %get-tuple-element.24.p_all, ...), custom_call_target="tpu_custom_call" | custom-call | tf_op jit(solution)/shard_map/experts/pallas_call | solution.py:354
  26.7 2.0 %pair.1 = (f32[64,1024]{1,0:T(8,128)S(1)}, f32[64,1024]{1,0:T(8,128)S(1)}) custom-call(f32[4,64,1024]{2,1,0:T(8,128)S(1)} %get-tuple-element.32.part), custom_call_target="tpu_custom_call" | custom-call | tf_op jit(solution)/shard_map/pair/pallas_call | solution.py:369
  28.7 1.3 %collective-permute-start = (f32[64,1024]{1,0:T(8,128)S(1)}, f32[64,1024]{1,0:T(8,128)S(1)}, u32[]{:S(2)}, u32[]{:S(2)}) collective-permute-start(f32[64,1024]{1,0:T(8,128)S(1)} %get-tuple-element.34), channel_id=1, source_target_pairs={{0,2},{1,3},{2,0},{3,1},{4,6},{5,7},{6,4},{7,5}} | collective-permute-start | bytes 786440 | tf_op jit(solution)/shard_map/ppermute | solution.py:378
  30.0 7.0 %rest.1 = (f32[8,1024,512]{2,1,0:T(8,128)}, f32[8,1024,512]{2,1,0:T(8,128)}, f32[8,512,1024]{2,1,0:T(8,128)}) custom-call(bf16[8,96,1024]{2,1,0:T(8,128)(2,1)S(1)} %get-tuple-element.25.x_all, bf16[8,96,1024]{2,1,0:T(8,128)(2,1)S(1)} %get-tuple-element.26.dz_all, ...), custom_call_target="tpu_custom_call", output_to_operand_aliasing={{0}: (5, {}), {1}: (6, {}), {2}: (7, {})} | custom-call | flops 905969664 | bytes 24379392 | tf_op jit(solution)/shard_map/rest/pallas_call | solution.py:380
  37.1 0.1 collective-permute-done
  37.1 0.7 %add_convert_fusion = bf16[64,1024]{1,0:T(8,128)(2,1)} fusion(f32[64,1024]{1,0:T(8,128)S(1)} %get-tuple-element.33, f32[64,1024]{1,0:T(8,128)S(1)} %collective-permute-done), kind=kLoop, calls=%fused_computation | loop fusion | flops 131072 | bytes 655360 | tf_op jit(solution)/shard_map/convert_element_type | solution.py:391
Async XLA Ops:
  28.7 8.4 %collective-permute-start = (f32[64,1024]{1,0:T(8,128)S(1)}, f32[64,1024]{1,0:T(8,128)S(1)}, u32[]{:S(2)}, u32[]{:S(2)}) collective-permute-start(f32[64,1024]{1,0:T(8,128)S(1)} %get-tuple-element.34), channel_id=1, source_target_pairs={{0,2},{1,3},{2,0},{3,1},{4,6},{5,7},{6,4},{7,5}} | collective-permute-start | bytes 786440 | tf_op jit(solution)/shard_map/ppermute | solution.py:378
